TPU v7x, 32 devices: a whole 2x2x4 slice. The times are simulated.
32 devices in a mesh: row: 8 (over z, x), col: 4 (over y, core).
Axes of the slice: x: 2, y: 2, z: 4, core: 2. Of those that a mesh axis runs over, the one named last changes fastest.
Arguments:
- tile_values: bfloat16 [192, 512, 128], P('row', 'col'), may hold values from -0.0546875 to 0.0546875
- tile_counts: int32 [96, 4], P('row', 'col'), may hold values from 0 to 2, as said below
- tile_cols: int32 [192, 4], P('row', 'col'), may hold values from 0 to 1, as said below
- panels: bfloat16 [12288, 4096], P('row', 'col'), may hold values from -6 to 6
Outputs:
- product: bfloat16 [1024, 4096], P('col', 'row')
Inputs may be any that keep to these rules, and one draw needn't show every extreme that they name: `tile_counts`: within each device the filled slots follow block row order; a device holds at most 24 tiles and some device holds exactly 24 in every draw. `tile_cols`: within one block row of a device the filled slots' columns rise strictly; entries of unfilled slots carry no meaning.
All inputs are finite; a program needn't handle non-finite values.
Results may differ from a plain program's by a relative error of at most 0.001.
Values may be sent and summed in bfloat16 or wider, within the bound.
A program may use at most 64 MiB of HBM per device.

v0:
```python
import functools

import jax
import jax.numpy as jnp
from jax import lax
from jax.experimental import pallas as pl
from jax.experimental.pallas import tpu as pltpu
from jax.sharding import PartitionSpec as P

BC_DEV = 2
PAIR = 2
BEHIND = 2
TOP = 32767.0
MESH = pl.DeviceIdType.MESH


def encode(value_ref, code_ref, step_ref):
    value = value_ref[...]
    peak = jnp.maximum(jnp.max(jnp.abs(value), axis=0, keepdims=True), 1e-30)
    code_ref[...] = jnp.round(value * (TOP / peak)).astype(jnp.int32).astype(jnp.int16)
    step_ref[...] = peak * (1.0 / TOP)


def decode(code_ref, step_ref):
    return code_ref[...].astype(jnp.int32).astype(jnp.float32) * step_ref[...]


def build_dense(counts_ref, cols_ref, tiles_ref, at_ref):
    slots, tile, _ = tiles_ref.shape
    start = jnp.int32(0)
    for i in range(counts_ref.shape[1]):
        count = counts_ref[0, i]
        here = jnp.minimum(start, slots - 1)
        after = jnp.minimum(start + 1, slots - 1)
        for j in range(BC_DEV):
            one = (count > 0) & (cols_ref[0, here] == j)
            two = (count > 1) & (cols_ref[0, after] == j)
            block = tiles_ref[jnp.where(two, after, here)]
            keep = jnp.where(one | two, 1.0, 0.0).astype(jnp.float32)
            block = (block.astype(jnp.float32) * keep).T.astype(jnp.bfloat16)
            at_ref[2 * j, :, i * tile : (i + 1) * tile] = block
        start = start + count


def kernel(
    n_row, n_col, counts_ref, cols_ref, tiles_ref, b_ref, o_ref,
    at_ref, away_ref, total_ref, own_ref, xs, xr, zs, zup, zdn, fin_ref, land_ref,
    at_send, at_recv, fw_send, x_send, x_recv, z_send, up_recv, dn_recv, f_send, f_recv,
):
    row, col = lax.axis_index("row"), lax.axis_index("col")
    n_z, n_y = n_row // PAIR, n_col // PAIR
    chunks = 2 * n_col
    z, x = row // PAIR, lax.rem(row, PAIR)
    y, k = col // PAIR, lax.rem(col, PAIR)
    wide = b_ref.shape[1] // PAIR

    def row_of(z_at, x_at):
        return z_at * PAIR + x_at

    def col_of(y_at, k_at):
        return y_at * PAIR + k_at

    beside = (row_of(z, 1 - x), col)
    above = (row_of(lax.rem(z + 1, n_z), x), col)
    below = (row_of(lax.rem(z + n_z - 1, n_z), x), col)
    partner = (row, col_of(y, 1 - k))

    barrier = pltpu.get_barrier_semaphore()
    for other in (beside, above, below):
        pl.semaphore_signal(barrier, inc=1, device_id=other, device_id_type=MESH)
    for step in range(1, n_col):
        pl.semaphore_signal(
            barrier, inc=1, device_id=(row, lax.rem(col + step, n_col)), device_id_type=MESH
        )
    build_dense(counts_ref, cols_ref, tiles_ref, at_ref)
    pl.semaphore_wait(barrier, 3 + n_col - 1)

    def copy(src, dst, send, recv, device):
        return pltpu.make_async_remote_copy(
            src_ref=src, dst_ref=dst, send_sem=send, recv_sem=recv,
            device_id=device, device_id_type=MESH,
        )

    first = []
    for j in range(BC_DEV):
        first.append(copy(at_ref.at[2 * j], at_ref.at[2 * j + 1], at_send.at[j],
                          at_recv.at[2 * j + 1], partner))
        for dy in range(1, n_y):
            to = (row, col_of(lax.rem(y + n_y - dy, n_y), k))
            slot = dy * 4 + 2 * j
            first.append(copy(at_ref.at[2 * j], at_ref.at[slot], at_send.at[dy * 2 + j],
                              at_recv.at[slot], to))
    for c in first:
        c.start()

    def forward(i):
        return copy(at_ref.at[i], at_ref.at[i + 1], fw_send.at[i], at_recv.at[i + 1], partner)

    class Both:
        def __init__(self, src, dst, send, recv, i, device):
            self.parts = [
                copy(src[t].at[i], dst[t].at[i], send.at[t, i], recv.at[t, i], device)
                for t in range(2)
            ]

        def start(self):
            for part in self.parts:
                part.start()

        def wait_send(self):
            for part in self.parts:
                part.wait_send()

        def wait_recv(self):
            for part in self.parts:
                part.wait_recv()

    def x_copy(i):
        return Both(xs, xr, x_send, x_recv, i, beside)

    def down_copy(i):
        return Both(zs, zup, z_send, up_recv, i, below)

    def up_copy(i):
        return Both(zs, zdn, z_send, dn_recv, i, above)

    def owner(i):
        dy, kk = i // 4, lax.rem(i, 2)
        return (row, col_of(lax.rem(y + dy, n_y), lax.rem(k + kk, PAIR)))

    def fin_copy(i):
        j = lax.rem(i, 4) // 2
        return copy(fin_ref.at[i], land_ref.at[j], f_send.at[i], f_recv.at[j], owner(i))

    def mine(i):
        return (i // 4 == 0) & (lax.rem(i, 2) == 0)

    def compute(i):
        @pl.when(jnp.logical_not(mine(i)))
        def _():
            copy(at_ref.at[i], at_ref.at[i], fw_send.at[i], at_recv.at[i], partner).wait_recv()

        @pl.when((i // 4 > 0) & (lax.rem(i, 2) == 0))
        def _():
            forward(i).start()

        lhs = at_ref[i]
        away = pl.ds(pl.multiple_of((1 - x) * wide, wide), wide)
        away_ref[...] = jnp.dot(lhs, b_ref[:, away], preferred_element_type=jnp.float32)
        encode(away_ref, xs[0].at[i], xs[1].at[i])
        x_copy(i).start()
        here = pl.ds(pl.multiple_of(x * wide, wide), wide)
        own_ref[i] = jnp.dot(lhs, b_ref[:, here], preferred_element_type=jnp.float32)

    final = z == col

    def combine(i):
        x_copy(i).wait_recv()
        total_ref[...] = own_ref[i] + decode(xr[0].at[i], xr[1].at[i])

        @pl.when((z >= col) & (z < n_z - 1))
        def _():
            down_copy(i).wait_recv()
            total_ref[...] += decode(zup[0].at[i], zup[1].at[i])

        @pl.when((z <= col) & (z > 0))
        def _():
            up_copy(i).wait_recv()
            total_ref[...] += decode(zdn[0].at[i], zdn[1].at[i])

        @pl.when(jnp.logical_not(final))
        def _():
            encode(total_ref, zs[0].at[i], zs[1].at[i])

        @pl.when(z > col)
        def _():
            down_copy(i).start()

        @pl.when(z < col)
        def _():
            up_copy(i).start()

        @pl.when(final)
        def _():
            fin_ref[i] = total_ref[...].astype(jnp.bfloat16)

            @pl.when(jnp.logical_not(mine(i)))
            def _():
                fin_copy(i).start()

    def main(i, carry):
        @pl.when(i < chunks)
        def _():
            compute(i)

        @pl.when(i >= BEHIND)
        def _():
            combine(i - BEHIND)

        return carry

    lax.fori_loop(0, chunks + BEHIND, main, 0)

    rows = land_ref.shape[1]
    for j in range(BC_DEV):
        @pl.when(final)
        def _(j=j):
            o_ref[j * rows : (j + 1) * rows] = fin_ref[2 * j]

        @pl.when(jnp.logical_not(final))
        def _(j=j):
            copy(fin_ref.at[2 * j], land_ref.at[j], f_send.at[2 * j], f_recv.at[j],
                 partner).wait_recv()
            o_ref[j * rows : (j + 1) * rows] = land_ref[j]

    for c in first:
        c.wait_send()

    def drain(i, carry):
        x_copy(i).wait_send()

        @pl.when((i // 4 > 0) & (lax.rem(i, 2) == 0))
        def _():
            forward(i).wait_send()

        @pl.when(jnp.logical_not(final))
        def _():
            down_copy(i).wait_send()

        @pl.when(final & jnp.logical_not(mine(i)))
        def _():
            fin_copy(i).wait_send()

        return carry

    lax.fori_loop(0, chunks, drain, 0)


def per_device(n_row, n_col, tile_values, tile_counts, tile_cols, panels):
    tile = tile_values.shape[1]
    deep, columns = panels.shape
    wide = columns // PAIR
    chunks = BC_DEV * n_col
    f32, bf16 = jnp.float32, jnp.bfloat16
    vmem = pl.BlockSpec(memory_space=pltpu.VMEM)
    smem = pl.BlockSpec(memory_space=pltpu.SMEM)
    dma = pltpu.SemaphoreType.DMA
    coded = (pltpu.VMEM((chunks, tile, wide), jnp.int16), pltpu.VMEM((chunks, 1, wide), f32))
    return pl.pallas_call(
        functools.partial(kernel, n_row, n_col),
        out_shape=jax.ShapeDtypeStruct((BC_DEV * tile, wide), bf16),
        in_specs=[smem, smem, vmem, vmem],
        out_specs=vmem,
        scratch_shapes=[
            pltpu.VMEM((chunks, tile, deep), bf16),
            pltpu.VMEM((tile, wide), f32),
            pltpu.VMEM((tile, wide), f32),
            pltpu.VMEM((chunks, tile, wide), f32),
            coded,
            coded,
            coded,
            coded,
            coded,
            pltpu.VMEM((chunks, tile, wide), bf16),
            pltpu.VMEM((BC_DEV, tile, wide), bf16),
            dma((n_col,)),
            dma((chunks,)),
            dma((chunks,)),
            dma((2, chunks)),
            dma((2, chunks)),
            dma((2, chunks)),
            dma((2, chunks)),
            dma((2, chunks)),
            dma((chunks,)),
            dma((BC_DEV,)),
        ],
        compiler_params=pltpu.CompilerParams(
            collective_id=0, has_side_effects=True, vmem_limit_bytes=56 * 1024 * 1024
        ),
    )(tile_counts.T, tile_cols.T, tile_values, panels)


def solution(mesh):
    n_row, n_col = mesh.shape["row"], mesh.shape["col"]
    return jax.shard_map(
        functools.partial(per_device, n_row, n_col),
        mesh=mesh,
        in_specs=(P("row", "col", None), P("row", "col"), P("row", "col"), P("row", "col")),
        out_specs=P("col", "row"),
        check_vma=False,
    )
```

profile of v0, /device:TPU:5, one launch (start us, length us, event | category | flops | bytes accessed | tf_op | source)
XLA Modules:
  0.0 53.2 jit_solution(2722554405306054197)
XLA Ops:
  0.0 51.6 %shard_map.46 = bf16[256,512]{1,0:T(8,128)(2,1)} custom-call(s32[1,12]{1,0:T(1,128)} %bitcast.2, s32[1,24]{1,0:T(1,128)} %bitcast.3, bf16[24,128,128]{2,1,0:T(8,128)(2,1)} %tiles_ref.1, bf16[1536,1024]{1,0:T(8,128)(2,1)} %b_ref.1), custom_call_target="tpu_custom_call" | custom-call | tf_op jit(solution)/shard_map/pallas_call | solution.py:249
  51.6 1.7 %copy.6 = bf16[256,512]{1,0:T(8,128)(2,1)} copy(bf16[256,512]{1,0:T(8,128)(2,1)} %shard_map.46) | data formatting | bytes 524288
where the time goes:
time: 53.8 us; the launch traced here: 53.2 us
  Pallas kernels  51.6 us (96%)
  local copies, waits for them, and re-layouts  1.67 us (3%)
    pallas_call x1, Pallas kernels, per_device(): pl.pallas_call(functools.partial(kernel, n_row, n_col), out_shape=jax.Sha...  51.6 us
    unnamed x1, local copies, waits for them, and re-layouts  1.67 us

commit v1 on v0

v1 whole, which is shorter than its diff:
```python
import functools

import jax
import jax.numpy as jnp
from jax import lax
from jax.experimental import pallas as pl
from jax.experimental.pallas import tpu as pltpu
from jax.sharding import PartitionSpec as P

BC_DEV = 2
PAIR = 2
SUB = 2
LAG_OUTER = 2
LAG_INNER = 5
LAG_FINAL = 8
TOP = 32767.0
MESH = pl.DeviceIdType.MESH
SELF, SIDE, FAR, FAR_SIDE = range(4)


def chunk_order(n_y):
    pieces = BC_DEV * SUB
    near = [(SELF, 0, p) for p in range(pieces)] + [(SIDE, 0, p) for p in range(pieces)]
    order, near = near[: pieces + 1], near[pieces + 1 :]
    for p in range(pieces):
        for dy in range(1, n_y):
            order += [(FAR, dy, p), (FAR_SIDE, dy, p)]
            if len(near) > 1:
                order.append(near.pop(0))
    return order + near


def pick(i, values):
    out = jnp.int32(values[0])
    for t, v in enumerate(values):
        if v != values[0]:
            out = jnp.where(i == t, jnp.int32(v), out)
    return out


def encode(value, code_ref, step_ref):
    peak = jnp.maximum(jnp.max(jnp.abs(value), axis=0, keepdims=True), 1e-30)
    code_ref[...] = jnp.round(value * (TOP / peak)).astype(jnp.int32).astype(jnp.int16)
    step_ref[...] = peak * (1.0 / TOP)


def decode(code_ref, step_ref):
    return code_ref[...].astype(jnp.int32).astype(jnp.float32) * step_ref[...]


def build_dense(j, counts_ref, cols_ref, tiles_ref, at_ref):
    slots, tile, _ = tiles_ref.shape
    half = tile // SUB
    start = jnp.int32(0)
    for i in range(counts_ref.shape[1]):
        count = counts_ref[0, i]
        here = jnp.minimum(start, slots - 1)
        after = jnp.minimum(start + 1, slots - 1)
        one = (count > 0) & (cols_ref[0, here] == j)
        two = (count > 1) & (cols_ref[0, after] == j)
        block = tiles_ref[jnp.where(two, after, here)]
        keep = jnp.where(one | two, 1.0, 0.0).astype(jnp.float32)
        block = (block.astype(jnp.float32) * keep).T.astype(jnp.bfloat16)
        for h in range(SUB):
            at_ref[SUB * j + h, :, i * tile : (i + 1) * tile] = block[h * half : (h + 1) * half]
        start = start + count


def kernel(
    n_row, n_col, counts_ref, cols_ref, tiles_hbm, b_hbm, o_ref,
    tiles_ref, b_away, b_own, at_ref, total_ref, own_ref, xs, xr, zs, zup, zdn, zsk,
    fin_ref, land_ref, load_sem,
    at_send, at_recv, fw_send, x_send, x_recv, z_send, up_recv, dn_recv, sk_recv, f_send, f_recv,
):
    row, col = lax.axis_index("row"), lax.axis_index("col")
    n_z, n_y = n_row // PAIR, n_col // PAIR
    order = chunk_order(n_y)
    chunks, pieces = len(order), BC_DEV * SUB
    z, x = row // PAIR, lax.rem(row, PAIR)
    y, k = col // PAIR, lax.rem(col, PAIR)
    wide = b_own.shape[1]
    place = {c: i for i, c in enumerate(order)}

    def row_of(z_at, x_at):
        return z_at * PAIR + x_at

    def col_of(y_at, k_at):
        return y_at * PAIR + k_at

    def load(src, dst, i):
        return pltpu.make_async_copy(src, dst, load_sem.at[i])

    at_away = pl.ds(pl.multiple_of((1 - x) * wide, wide), wide)
    at_own = pl.ds(pl.multiple_of(x * wide, wide), wide)
    loads = [
        load(tiles_hbm, tiles_ref, 0),
        load(b_hbm.at[:, at_away], b_away, 1),
        load(b_hbm.at[:, at_own], b_own, 2),
    ]
    for c in loads:
        c.start()

    beside = (row_of(z, 1 - x), col)
    partner = (row, col_of(y, 1 - k))
    final = z == col
    even = k == 0
    skip_up = even & (z == col + 2)
    skip_dn = jnp.logical_not(even) & (z == col - 2)
    skips = skip_up | skip_dn
    goes_down = (z > col) & jnp.logical_not(skip_up)
    goes_up = (z < col) & jnp.logical_not(skip_dn)
    from_above = (z >= col) & (z < n_z - 1) & jnp.logical_not(even & (z == col + 1))
    from_below = (z <= col) & (z > 0) & jnp.logical_not(jnp.logical_not(even) & (z == col - 1))
    from_skip = final & ((even & (col + 2 < n_z)) | (jnp.logical_not(even) & (col >= 2)))
    above = (row_of(jnp.minimum(z + 1, n_z - 1), x), col)
    below = (row_of(jnp.maximum(z - 1, 0), x), col)
    skip_to = (row_of(jnp.minimum(col, n_z - 1), x), col)
    skip_of = (row_of(jnp.clip(jnp.where(even, col + 2, col - 2), 0, n_z - 1), x), col)

    def flag(b):
        return jnp.where(b, 1, 0).astype(jnp.int32)

    barrier = pltpu.get_barrier_semaphore()

    def greet(device):
        pl.semaphore_signal(barrier, inc=1, device_id=device, device_id_type=MESH)

    greet(beside)
    for step in range(1, n_col):
        greet((row, lax.rem(col + step, n_col)))
    pl.when(z < n_z - 1)(lambda: greet(above))
    pl.when(z > 0)(lambda: greet(below))
    pl.when(skips)(lambda: greet(skip_to))
    pl.when(from_skip)(lambda: greet(skip_of))

    def copy(src, dst, send, recv, device):
        return pltpu.make_async_remote_copy(
            src_ref=src, dst_ref=dst, send_sem=send, recv_sem=recv,
            device_id=device, device_id_type=MESH,
        )

    loads[0].wait()
    first = []
    for j in range(BC_DEV):
        build_dense(j, counts_ref, cols_ref, tiles_ref, at_ref)
        if j == 0:
            pl.semaphore_wait(
                barrier, n_col + flag(z < n_z - 1) + flag(z > 0) + flag(skips) + flag(from_skip)
            )
        for p in range(j * SUB, (j + 1) * SUB):
            here = place[(SELF, 0, p)]
            assert here == p
            for dy in range(1, n_y):
                to = (row, col_of(lax.rem(y + n_y - dy, n_y), k))
                there = place[(FAR, dy, p)]
                first.append(copy(at_ref.at[here], at_ref.at[there], at_send.at[dy * pieces + p],
                                  at_recv.at[there], to))
                first[-1].start()
            there = place[(SIDE, 0, p)]
            first.append(copy(at_ref.at[here], at_ref.at[there], at_send.at[p],
                              at_recv.at[there], partner))
            first[-1].start()

    kinds, dys, ps = ([c[t] for c in order] for t in range(3))

    def forward(i):
        return copy(at_ref.at[i], at_ref.at[i + 1], fw_send.at[i], at_recv.at[i + 1], partner)

    class Both:
        def __init__(self, src, dst, send, recv, i, device):
            self.parts = [
                copy(src[t].at[i], dst[t].at[i], send.at[t, i], recv.at[t, i], device)
                for t in range(2)
            ]

        def start(self):
            for part in self.parts:
                part.start()

        def wait_send(self):
            for part in self.parts:
                part.wait_send()

        def wait_recv(self):
            for part in self.parts:
                part.wait_recv()

    def x_copy(i):
        return Both(xs, xr, x_send, x_recv, i, beside)

    def down_copy(i):
        return Both(zs, zup, z_send, up_recv, i, below)

    def up_copy(i):
        return Both(zs, zdn, z_send, dn_recv, i, above)

    def skip_copy(i):
        return Both(zs, zsk, z_send, sk_recv, i, skip_to)

    def fin_copy(i):
        kind, dy, p = pick(i, kinds), pick(i, dys), pick(i, ps)
        odd = lax.rem(kind, 2)
        to = (row, col_of(lax.rem(y + dy, n_y), lax.rem(k + odd, PAIR)))
        return copy(fin_ref.at[i], land_ref.at[p], f_send.at[i], f_recv.at[p], to)

    def compute(i):
        kind = pick(i, kinds)

        @pl.when(kind != SELF)
        def _():
            copy(at_ref.at[i], at_ref.at[i], fw_send.at[i], at_recv.at[i], partner).wait_recv()

        @pl.when(kind == FAR)
        def _():
            forward(i).start()

        lhs = at_ref[i]
        encode(jnp.dot(lhs, b_away[...], preferred_element_type=jnp.float32), xs[0].at[i], xs[1].at[i])
        x_copy(i).start()
        own_ref[i] = jnp.dot(lhs, b_own[...], preferred_element_type=jnp.float32)

    def combine(i):
        x_copy(i).wait_recv()
        total_ref[...] = own_ref[i] + decode(xr[0].at[i], xr[1].at[i])

        @pl.when(from_above)
        def _():
            down_copy(i).wait_recv()
            total_ref[...] += decode(zup[0].at[i], zup[1].at[i])

        @pl.when(from_below)
        def _():
            up_copy(i).wait_recv()
            total_ref[...] += decode(zdn[0].at[i], zdn[1].at[i])

        @pl.when(from_skip)
        def _():
            skip_copy(i).wait_recv()
            total_ref[...] += decode(zsk[0].at[i], zsk[1].at[i])

        @pl.when(jnp.logical_not(final))
        def _():
            encode(total_ref[...], zs[0].at[i], zs[1].at[i])

        @pl.when(goes_down)
        def _():
            down_copy(i).start()

        @pl.when(goes_up)
        def _():
            up_copy(i).start()

        @pl.when(skips)
        def _():
            skip_copy(i).start()

        @pl.when(final)
        def _():
            fin_ref[i] = total_ref[...].astype(jnp.bfloat16)

            @pl.when(pick(i, kinds) != SELF)
            def _():
                fin_copy(i).start()

    inner = jnp.logical_not(final) & (from_above | from_below)
    lag = jnp.where(final, LAG_FINAL, jnp.where(inner, LAG_INNER, LAG_OUTER))

    loads[1].wait()
    loads[2].wait()

    def main(i, carry):
        @pl.when(i < chunks)
        def _():
            compute(i)

        @pl.when((i >= lag) & (i < chunks + lag))
        def _():
            combine(i - lag)

        return carry

    lax.fori_loop(0, chunks + LAG_FINAL, main, 0)

    rows = land_ref.shape[1]
    for p in range(pieces):
        @pl.when(final)
        def _(p=p):
            o_ref[p * rows : (p + 1) * rows] = fin_ref[p]

        @pl.when(jnp.logical_not(final))
        def _(p=p):
            copy(fin_ref.at[p], land_ref.at[p], f_send.at[p], f_recv.at[p], partner).wait_recv()
            o_ref[p * rows : (p + 1) * rows] = land_ref[p]

    for c in first:
        c.wait_send()

    def drain(i, carry):
        x_copy(i).wait_send()

        @pl.when(pick(i, kinds) == FAR)
        def _():
            forward(i).wait_send()

        @pl.when(jnp.logical_not(final))
        def _():
            down_copy(i).wait_send()

        @pl.when(final & (pick(i, kinds) != SELF))
        def _():
            fin_copy(i).wait_send()

        return carry

    lax.fori_loop(0, chunks, drain, 0)


def per_device(n_row, n_col, tile_values, tile_counts, tile_cols, panels):
    slots, tile, _ = tile_values.shape
    deep, columns = panels.shape
    wide = columns // PAIR
    pieces = BC_DEV * SUB
    chunks = pieces * n_col
    rows = tile // SUB
    f32, bf16 = jnp.float32, jnp.bfloat16
    vmem = pl.BlockSpec(memory_space=pltpu.VMEM)
    smem = pl.BlockSpec(memory_space=pltpu.SMEM)
    hbm = pl.BlockSpec(memory_space=pl.ANY)
    dma = pltpu.SemaphoreType.DMA
    coded = (pltpu.VMEM((chunks, rows, wide), jnp.int16), pltpu.VMEM((chunks, 1, wide), f32))
    return pl.pallas_call(
        functools.partial(kernel, n_row, n_col),
        out_shape=jax.ShapeDtypeStruct((BC_DEV * tile, wide), bf16),
        in_specs=[smem, smem, hbm, hbm],
        out_specs=vmem,
        scratch_shapes=[
            pltpu.VMEM((slots, tile, tile), bf16),
            pltpu.VMEM((deep, wide), bf16),
            pltpu.VMEM((deep, wide), bf16),
            pltpu.VMEM((chunks, rows, deep), bf16),
            pltpu.VMEM((rows, wide), f32),
            pltpu.VMEM((chunks, rows, wide), f32),
            coded,
            coded,
            coded,
            coded,
            coded,
            coded,
            pltpu.VMEM((chunks, rows, wide), bf16),
            pltpu.VMEM((pieces, rows, wide), bf16),
            dma((3,)),
            dma((n_col // PAIR * pieces,)),
            dma((chunks,)),
            dma((chunks,)),
            dma((2, chunks)),
            dma((2, chunks)),
            dma((2, chunks)),
            dma((2, chunks)),
            dma((2, chunks)),
            dma((2, chunks)),
            dma((chunks,)),
            dma((pieces,)),
        ],
        compiler_params=pltpu.CompilerParams(
            collective_id=0, has_side_effects=True, vmem_limit_bytes=56 * 1024 * 1024
        ),
    )(tile_counts.T, tile_cols.T, tile_values, panels)


def solution(mesh):
    n_row, n_col = mesh.shape["row"], mesh.shape["col"]
    return jax.shard_map(
        functools.partial(per_device, n_row, n_col),
        mesh=mesh,
        in_specs=(P("row", "col", None), P("row", "col"), P("row", "col"), P("row", "col")),
        out_specs=P("col", "row"),
        check_vma=False,
    )
```

time: 53.8 us -> 46.6 us (0.87)
  Pallas kernels: 51.6 us -> 44.5 us
    pallas_call x1, Pallas kernels: 51.6 us -> 44.5 us  [per_device(): pl.pallas_call(functools.partial(kernel, n_row, n_col), out_shape=jax.Sha...]
where the time goes in v1:
time: 46.6 us; the launch traced here: 46.1 us
  Pallas kernels  44.5 us (95%)
  local copies, waits for them, and re-layouts  1.67 us (4%)
    pallas_call x1, Pallas kernels, per_device(): pl.pallas_call(functools.partial(kernel, n_row, n_col), out_shape=jax.Sha...  44.5 us
    unnamed x1, local copies, waits for them, and re-layouts  1.67 us

profile of v1, /device:TPU:5, one launch (start us, length us, event | category | flops | bytes accessed | tf_op | source)
XLA Modules:
  0.0 46.1 jit_solution(2804936438439395424)
XLA Ops:
  0.0 44.5 %shard_map.46 = bf16[256,512]{1,0:T(8,128)(2,1)} custom-call(s32[1,12]{1,0:T(1,128)} %bitcast.2, s32[1,24]{1,0:T(1,128)} %bitcast.3, bf16[24,128,128]{2,1,0:T(8,128)(2,1)} %tiles_hbm.1, bf16[1536,1024]{1,0:T(8,128)(2,1)} %b_hbm.1), custom_call_target="tpu_custom_call" | custom-call | tf_op jit(solution)/shard_map/pallas_call | solution.py:331
  44.5 1.7 %copy.6 = bf16[256,512]{1,0:T(8,128)(2,1)} copy(bf16[256,512]{1,0:T(8,128)(2,1)} %shard_map.46) | data formatting | bytes 524288

commit v2 on v1

--- a/solution.py
+++ b/solution.py
@@ -68,9 +68,9 @@
 
 def kernel(
     n_row, n_col, counts_ref, cols_ref, tiles_hbm, b_hbm, o_ref,
-    tiles_ref, b_away, b_own, at_ref, total_ref, own_ref, xs, xr, zs, zup, zdn, zsk,
-    fin_ref, land_ref, load_sem,
-    at_send, at_recv, fw_send, x_send, x_recv, z_send, up_recv, dn_recv, sk_recv, f_send, f_recv,
+    tiles_ref, b_away, b_own, at_ref, total_ref, own_ref, xs, xr, zs, zup, zdn,
+    fin_ref, land_ref, size_ref, load_sem,
+    at_send, at_recv, fw_send, x_send, x_recv, z_send, up_recv, dn_recv, f_send, f_recv, out_sem,
 ):
     row, col = lax.axis_index("row"), lax.axis_index("col")
     n_z, n_y = n_row // PAIR, n_col // PAIR
@@ -103,19 +103,19 @@
     beside = (row_of(z, 1 - x), col)
     partner = (row, col_of(y, 1 - k))
     final = z == col
-    even = k == 0
-    skip_up = even & (z == col + 2)
-    skip_dn = jnp.logical_not(even) & (z == col - 2)
+    skip_up = (col == 0) & (z == 2)
+    skip_dn = (col == n_z - 1) & (z == n_z - 3)
     skips = skip_up | skip_dn
     goes_down = (z > col) & jnp.logical_not(skip_up)
     goes_up = (z < col) & jnp.logical_not(skip_dn)
-    from_above = (z >= col) & (z < n_z - 1) & jnp.logical_not(even & (z == col + 1))
-    from_below = (z <= col) & (z > 0) & jnp.logical_not(jnp.logical_not(even) & (z == col - 1))
-    from_skip = final & ((even & (col + 2 < n_z)) | (jnp.logical_not(even) & (col >= 2)))
+    low_end, high_end = (z == 0) & (col == 0), (z == n_z - 1) & (col == n_z - 1)
+    from_above = (z >= col) & (z < n_z - 1) & jnp.logical_not((col == 0) & (z == 1)) | high_end
+    from_below = (z <= col) & (z > 0) & jnp.logical_not((col == n_z - 1) & (z == n_z - 2)) | low_end
+    from_skip = low_end | high_end
     above = (row_of(jnp.minimum(z + 1, n_z - 1), x), col)
     below = (row_of(jnp.maximum(z - 1, 0), x), col)
     skip_to = (row_of(jnp.minimum(col, n_z - 1), x), col)
-    skip_of = (row_of(jnp.clip(jnp.where(even, col + 2, col - 2), 0, n_z - 1), x), col)
+    skip_of = (row_of(jnp.where(low_end, 2, n_z - 3), x), col)
 
     def flag(b):
         return jnp.where(b, 1, 0).astype(jnp.int32)
@@ -139,120 +139,104 @@
             device_id=device, device_id_type=MESH,
         )
 
-    loads[0].wait()
+    with jax.named_scope("wait_tiles"):
+        loads[0].wait()
     first = []
     for j in range(BC_DEV):
-        build_dense(j, counts_ref, cols_ref, tiles_ref, at_ref)
+        with jax.named_scope("build"):
+            build_dense(j, counts_ref, cols_ref, tiles_ref, at_ref)
         if j == 0:
-            pl.semaphore_wait(
-                barrier, n_col + flag(z < n_z - 1) + flag(z > 0) + flag(skips) + flag(from_skip)
-            )
+            with jax.named_scope("wait_barrier"):
+                pl.semaphore_wait(
+                    barrier, n_col + flag(z < n_z - 1) + flag(z > 0) + flag(skips) + flag(from_skip)
+                )
         for p in range(j * SUB, (j + 1) * SUB):
             here = place[(SELF, 0, p)]
             assert here == p
             for dy in range(1, n_y):
                 to = (row, col_of(lax.rem(y + n_y - dy, n_y), k))
                 there = place[(FAR, dy, p)]
-                first.append(copy(at_ref.at[here], at_ref.at[there], at_send.at[dy * pieces + p],
+                first.append(copy(at_ref.at[here], at_ref.at[there], at_send.at[0],
                                   at_recv.at[there], to))
                 first[-1].start()
             there = place[(SIDE, 0, p)]
-            first.append(copy(at_ref.at[here], at_ref.at[there], at_send.at[p],
+            first.append(copy(at_ref.at[here], at_ref.at[there], at_send.at[0],
                               at_recv.at[there], partner))
             first[-1].start()
 
     kinds, dys, ps = ([c[t] for c in order] for t in range(3))
 
     def forward(i):
-        return copy(at_ref.at[i], at_ref.at[i + 1], fw_send.at[i], at_recv.at[i + 1], partner)
-
-    class Both:
-        def __init__(self, src, dst, send, recv, i, device):
-            self.parts = [
-                copy(src[t].at[i], dst[t].at[i], send.at[t, i], recv.at[t, i], device)
-                for t in range(2)
-            ]
-
-        def start(self):
-            for part in self.parts:
-                part.start()
-
-        def wait_send(self):
-            for part in self.parts:
-                part.wait_send()
-
-        def wait_recv(self):
-            for part in self.parts:
-                part.wait_recv()
-
-    def x_copy(i):
-        return Both(xs, xr, x_send, x_recv, i, beside)
-
-    def down_copy(i):
-        return Both(zs, zup, z_send, up_recv, i, below)
-
-    def up_copy(i):
-        return Both(zs, zdn, z_send, dn_recv, i, above)
-
-    def skip_copy(i):
-        return Both(zs, zsk, z_send, sk_recv, i, skip_to)
+        return copy(at_ref.at[i], at_ref.at[i + 1], fw_send.at[0], at_recv.at[i + 1], partner)
+
+    def send(src, dst, send_sem, recv_sem, i, device):
+        for t in range(2):
+            copy(src[t].at[i], dst[t].at[i], send_sem.at[0], recv_sem.at[i], device).start()
+
+    def take(recv_sem, i):
+        pltpu.make_async_copy(size_ref.at[i], size_ref.at[i], recv_sem.at[i]).wait()
 
     def fin_copy(i):
         kind, dy, p = pick(i, kinds), pick(i, dys), pick(i, ps)
         odd = lax.rem(kind, 2)
         to = (row, col_of(lax.rem(y + dy, n_y), lax.rem(k + odd, PAIR)))
-        return copy(fin_ref.at[i], land_ref.at[p], f_send.at[i], f_recv.at[p], to)
+        return copy(fin_ref.at[i], land_ref.at[p], f_send.at[0], f_recv.at[p], to)
 
     def compute(i):
         kind = pick(i, kinds)
 
-        @pl.when(kind != SELF)
-        def _():
-            copy(at_ref.at[i], at_ref.at[i], fw_send.at[i], at_recv.at[i], partner).wait_recv()
+        with jax.named_scope("wait_a"):
+            @pl.when(kind != SELF)
+            def _():
+                copy(at_ref.at[i], at_ref.at[i], fw_send.at[0], at_recv.at[i], partner).wait_recv()
 
         @pl.when(kind == FAR)
         def _():
             forward(i).start()
 
-        lhs = at_ref[i]
-        encode(jnp.dot(lhs, b_away[...], preferred_element_type=jnp.float32), xs[0].at[i], xs[1].at[i])
-        x_copy(i).start()
-        own_ref[i] = jnp.dot(lhs, b_own[...], preferred_element_type=jnp.float32)
+        with jax.named_scope("dot_away"):
+            lhs = at_ref[i]
+            encode(jnp.dot(lhs, b_away[...], preferred_element_type=jnp.float32), xs[0].at[i], xs[1].at[i])
+            send(xs, xr, x_send, x_recv, i, beside)
+        with jax.named_scope("dot_own"):
+            own_ref[i] = jnp.dot(lhs, b_own[...], preferred_element_type=jnp.float32)
 
     def combine(i):
-        x_copy(i).wait_recv()
+        with jax.named_scope("wait_x"):
+            take(x_recv, i)
         total_ref[...] = own_ref[i] + decode(xr[0].at[i], xr[1].at[i])
 
         @pl.when(from_above)
         def _():
-            down_copy(i).wait_recv()
+            with jax.named_scope("wait_up"):
+                take(up_recv, i)
             total_ref[...] += decode(zup[0].at[i], zup[1].at[i])
 
         @pl.when(from_below)
         def _():
-            up_copy(i).wait_recv()
+            with jax.named_scope("wait_dn"):
+                take(dn_recv, i)
             total_ref[...] += decode(zdn[0].at[i], zdn[1].at[i])
 
-        @pl.when(from_skip)
-        def _():
-            skip_copy(i).wait_recv()
-            total_ref[...] += decode(zsk[0].at[i], zsk[1].at[i])
-
         @pl.when(jnp.logical_not(final))
         def _():
             encode(total_ref[...], zs[0].at[i], zs[1].at[i])
 
         @pl.when(goes_down)
         def _():
-            down_copy(i).start()
+            send(zs, zup, z_send, up_recv, i, below)
 
         @pl.when(goes_up)
         def _():
-            up_copy(i).start()
-
-        @pl.when(skips)
-        def _():
-            skip_copy(i).start()
+            send(zs, zdn, z_send, dn_recv, i, above)
+
+        @pl.when(skip_up)
+        def _():
+            send(zs, zdn, z_send, dn_recv, i, skip_to)
+
+        @pl.when(skip_dn)
+        def _():
+            send(zs, zup, z_send, up_recv, i, skip_to)
 
         @pl.when(final)
         def _():
@@ -265,8 +249,9 @@
     inner = jnp.logical_not(final) & (from_above | from_below)
     lag = jnp.where(final, LAG_FINAL, jnp.where(inner, LAG_INNER, LAG_OUTER))
 
-    loads[1].wait()
-    loads[2].wait()
+    with jax.named_scope("wait_b"):
+        loads[1].wait()
+        loads[2].wait()
 
     def main(i, carry):
         @pl.when(i < chunks)
@@ -282,37 +267,39 @@
     lax.fori_loop(0, chunks + LAG_FINAL, main, 0)
 
     rows = land_ref.shape[1]
+
+    def out(src, p):
+        return pltpu.make_async_copy(src.at[p], o_ref.at[pl.ds(p * rows, rows)], out_sem.at[0])
+
     for p in range(pieces):
         @pl.when(final)
         def _(p=p):
-            o_ref[p * rows : (p + 1) * rows] = fin_ref[p]
+            out(fin_ref, p).start()
 
         @pl.when(jnp.logical_not(final))
         def _(p=p):
-            copy(fin_ref.at[p], land_ref.at[p], f_send.at[p], f_recv.at[p], partner).wait_recv()
-            o_ref[p * rows : (p + 1) * rows] = land_ref[p]
-
-    for c in first:
-        c.wait_send()
-
-    def drain(i, carry):
-        x_copy(i).wait_send()
-
-        @pl.when(pick(i, kinds) == FAR)
-        def _():
-            forward(i).wait_send()
+            with jax.named_scope("wait_land"):
+                copy(fin_ref.at[p], land_ref.at[p], f_send.at[0], f_recv.at[p], partner).wait_recv()
+            out(land_ref, p).start()
+
+    def drained(ref, sem):
+        pltpu.make_async_copy(ref, ref, sem.at[0]).wait()
+
+    with jax.named_scope("drain"):
+        drained(at_ref.at[pl.ds(0, n_y * pieces)], at_send)
+        drained(at_ref.at[pl.ds(0, (n_y - 1) * pieces)], fw_send)
+        drained(size_ref, x_send)
 
         @pl.when(jnp.logical_not(final))
         def _():
-            down_copy(i).wait_send()
-
-        @pl.when(final & (pick(i, kinds) != SELF))
-        def _():
-            fin_copy(i).wait_send()
-
-        return carry
-
-    lax.fori_loop(0, chunks, drain, 0)
+            drained(size_ref, z_send)
+
+        @pl.when(final)
+        def _():
+            drained(fin_ref.at[pl.ds(pieces, chunks - pieces)], f_send)
+
+    with jax.named_scope("wait_out"):
+        drained(o_ref, out_sem)
 
 
 def per_device(n_row, n_col, tile_values, tile_counts, tile_cols, panels):
@@ -323,7 +310,6 @@
     chunks = pieces * n_col
     rows = tile // SUB
     f32, bf16 = jnp.float32, jnp.bfloat16
-    vmem = pl.BlockSpec(memory_space=pltpu.VMEM)
     smem = pl.BlockSpec(memory_space=pltpu.SMEM)
     hbm = pl.BlockSpec(memory_space=pl.ANY)
     dma = pltpu.SemaphoreType.DMA
@@ -332,7 +318,7 @@
         functools.partial(kernel, n_row, n_col),
         out_shape=jax.ShapeDtypeStruct((BC_DEV * tile, wide), bf16),
         in_specs=[smem, smem, hbm, hbm],
-        out_specs=vmem,
+        out_specs=hbm,
         scratch_shapes=[
             pltpu.VMEM((slots, tile, tile), bf16),
             pltpu.VMEM((deep, wide), bf16),
@@ -345,21 +331,21 @@
             coded,
             coded,
             coded,
-            coded,
             pltpu.VMEM((chunks, rows, wide), bf16),
             pltpu.VMEM((pieces, rows, wide), bf16),
+            pltpu.VMEM((chunks, 1, (rows // 2 + 1) * wide), f32),
             dma((3,)),
-            dma((n_col // PAIR * pieces,)),
+            dma((1,)),
+            dma((chunks,)),
+            dma((1,)),
+            dma((1,)),
+            dma((chunks,)),
+            dma((1,)),
             dma((chunks,)),
             dma((chunks,)),
-            dma((2, chunks)),
-            dma((2, chunks)),
-            dma((2, chunks)),
-            dma((2, chunks)),
-            dma((2, chunks)),
-            dma((2, chunks)),
-            dma((chunks,)),
+            dma((1,)),
             dma((pieces,)),
+            dma((1,)),
         ],
         compiler_params=pltpu.CompilerParams(
             collective_id=0, has_side_effects=True, vmem_limit_bytes=56 * 1024 * 1024

time: 46.6 us -> 44.5 us (0.955)
  Pallas kernels: 44.5 us -> 42.4 us
    pallas_call x1, Pallas kernels: 44.5 us -> 42.4 us  [per_device(): pl.pallas_call(functools.partial(kernel, n_row, n_col), out_shape=jax.Sha...]
where the time goes in v2:
time: 44.5 us; the launch traced here: 44.1 us
  Pallas kernels  42.4 us (95%)
  local copies, waits for them, and re-layouts  1.67 us (4%)
    pallas_call x1, Pallas kernels, per_device(): pl.pallas_call(functools.partial(kernel, n_row, n_col), out_shape=jax.Sha...  42.4 us
    unnamed x1, local copies, waits for them, and re-layouts  1.67 us

profile of v2, /device:TPU:5, one launch (start us, length us, event | category | flops | bytes accessed | tf_op | source)
XLA Modules:
  0.0 44.1 jit_solution(6650826881387127873)
XLA Ops:
  0.0 42.4 %shard_map.46 = bf16[256,512]{1,0:T(8,128)(2,1)} custom-call(s32[1,12]{1,0:T(1,128)} %bitcast.2, s32[1,24]{1,0:T(1,128)} %bitcast.3, bf16[24,128,128]{2,1,0:T(8,128)(2,1)} %tiles_hbm.1, bf16[1536,1024]{1,0:T(8,128)(2,1)} %b_hbm.1), custom_call_target="tpu_custom_call" | custom-call | tf_op jit(solution)/shard_map/pallas_call | solution.py:317
  42.4 1.7 %copy.6 = bf16[256,512]{1,0:T(8,128)(2,1)} copy(bf16[256,512]{1,0:T(8,128)(2,1)} %shard_map.46) | data formatting | bytes 524288

commit v3 on v2

v3 whole, which is shorter than its diff:
```python
import functools

import jax
import jax.numpy as jnp
from jax import lax
from jax.experimental import pallas as pl
from jax.experimental.pallas import tpu as pltpu
from jax.sharding import PartitionSpec as P

BC_DEV = 2
PAIR = 2
PIECES = 4
Z_WAIT = 4
LAG_OUTER = 1
LAG_INNER = 3
LAG_FINAL = 7
TOP = 32767.0
MESH = pl.DeviceIdType.MESH


class Plan:
    def __init__(self, n_y):
        self.others = n_y - 1
        self.near = 2 * BC_DEV
        self.pairs = (PIECES - 1) * self.others
        self.tails = 2 * self.others
        self.slots = self.near + self.pairs
        self.units = 2 * self.slots + self.tails
        self.hops = self.units + 1
        self.arrivals = BC_DEV + 2 * (self.pairs + self.tails)


def encode(value, code_ref, step_ref):
    peak = jnp.maximum(jnp.max(jnp.abs(value), axis=0, keepdims=True), 1e-30)
    code_ref[...] = jnp.round(value * (TOP / peak)).astype(jnp.int32).astype(jnp.int16)
    step_ref[...] = peak * (1.0 / TOP)


def decode(code_ref, step_ref):
    return code_ref[...].astype(jnp.int32).astype(jnp.float32) * step_ref[...]


def build_dense(j, counts_ref, cols_ref, tiles_ref, at_ref):
    slots, tile, _ = tiles_ref.shape
    start = jnp.int32(0)
    for i in range(counts_ref.shape[1]):
        count = counts_ref[0, i]
        here = jnp.minimum(start, slots - 1)
        after = jnp.minimum(start + 1, slots - 1)
        one = (count > 0) & (cols_ref[0, here] == j)
        two = (count > 1) & (cols_ref[0, after] == j)
        block = tiles_ref[jnp.where(two, after, here)]
        keep = jnp.where(one | two, 1.0, 0.0).astype(jnp.float32)
        at_ref[j, :, i * tile : (i + 1) * tile] = (block.astype(jnp.float32) * keep).T.astype(jnp.bfloat16)
        start = start + count


def kernel(
    n_row, n_col, counts_hbm, cols_hbm, tiles_hbm, b_hbm, o_ref,
    counts_ref, cols_ref, tiles_ref, b_away, b_own, at_ref, tail_ref, own_ref, away_ref, xs, xr, zs, zr,
    fin_ref, land_ref, size_ref, load_sem,
    a_send, a_recv, fw_send, x_send, x_recv, z_send, z_recv, f_send, f_recv, out_sem,
):
    row, col = lax.axis_index("row"), lax.axis_index("col")
    n_z, n_y = n_row // PAIR, n_col // PAIR
    plan = Plan(n_y)
    z, x = row // PAIR, lax.rem(row, PAIR)
    y, k = col // PAIR, lax.rem(col, PAIR)
    wide = b_own.shape[1]
    rows = own_ref.shape[1]
    half = rows // 2

    def row_of(z_at, x_at):
        return z_at * PAIR + x_at

    def col_of(y_at, k_at):
        return y_at * PAIR + k_at

    def load(src, dst, i):
        return pltpu.make_async_copy(src, dst, load_sem.at[i])

    at_away = pl.ds(pl.multiple_of((1 - x) * wide, wide), wide)
    at_own = pl.ds(pl.multiple_of(x * wide, wide), wide)
    loads = [
        load(tiles_hbm, tiles_ref, 0),
        load(counts_hbm, counts_ref, 3),
        load(cols_hbm, cols_ref, 4),
        load(b_hbm.at[:, at_away], b_away, 1),
        load(b_hbm.at[:, at_own], b_own, 2),
    ]
    for c in loads:
        c.start()

    beside = (row_of(z, 1 - x), col)
    partner = (row, col_of(y, 1 - k))
    final = z == col
    skip_up = (col == 0) & (z == 2)
    skip_dn = (col == n_z - 1) & (z == n_z - 3)
    low_end, high_end = (z == 0) & (col == 0), (z == n_z - 1) & (col == n_z - 1)
    skips, from_skip = skip_up | skip_dn, low_end | high_end
    from_above = (z > col) & (z < n_z - 1) & jnp.logical_not((col == 0) & (z == 1))
    from_below = (z < col) & (z > 0) & jnp.logical_not((col == n_z - 1) & (z == n_z - 2))
    inner = from_above | from_below
    outer = jnp.logical_not(final | inner)
    from_side = jnp.where(z > col, 0, 1)
    to_side = jnp.where(skips, 1 - from_side, from_side)
    z_next = jnp.where(final, jnp.where(z < n_z - 1, z + 1, z - 1), jnp.where(z > col, z - 1, z + 1))
    z_next = jnp.where(skips, jnp.minimum(col, n_z - 1), z_next)
    onward = (row_of(z_next, x), col)
    above = (row_of(jnp.minimum(z + 1, n_z - 1), x), col)
    below = (row_of(jnp.maximum(z - 1, 0), x), col)
    skip_of = (row_of(jnp.where(low_end, 2, n_z - 3), x), col)

    def flag(b):
        return jnp.where(b, 1, 0).astype(jnp.int32)

    barrier = pltpu.get_barrier_semaphore()

    def greet(device):
        pl.semaphore_signal(barrier, inc=1, device_id=device, device_id_type=MESH)

    greet(beside)
    for step in range(1, n_col):
        greet((row, lax.rem(col + step, n_col)))
    pl.when(z < n_z - 1)(lambda: greet(above))
    pl.when(z > 0)(lambda: greet(below))
    pl.when(skips)(lambda: greet(onward))
    pl.when(from_skip)(lambda: greet(skip_of))

    def copy(src, dst, send, recv, device):
        return pltpu.make_async_remote_copy(
            src_ref=src, dst_ref=dst, send_sem=send, recv_sem=recv,
            device_id=device, device_id_type=MESH,
        )

    with jax.named_scope("wait_tiles"):
        for c in loads[:3]:
            c.wait()
    for j in range(BC_DEV):
        with jax.named_scope("build"):
            build_dense(j, counts_ref, cols_ref, tiles_ref, at_ref)
        if j == 0:
            with jax.named_scope("wait_barrier"):
                pl.semaphore_wait(
                    barrier, n_col + flag(z < n_z - 1) + flag(z > 0) + flag(skips) + flag(from_skip)
                )
        for p in range(2 * j, 2 * j + 2):
            at = p % 2 * rows
            for dy in range(1, n_y):
                to = (row, col_of(lax.rem(y + n_y - dy, n_y), k))
                if p < PIECES - 1:
                    q = p * plan.others + dy - 1
                    copy(at_ref.at[j, pl.ds(at, rows)], at_ref.at[plan.near + q, pl.ds(0, rows)],
                         a_send.at[0], a_recv.at[BC_DEV + 2 * q], to).start()
                    continue
                for h in range(2):
                    t = h * plan.others + dy - 1
                    copy(at_ref.at[j, pl.ds(at + h * half, half)], tail_ref.at[t, pl.ds(0, half)],
                         a_send.at[0], a_recv.at[BC_DEV + 2 * (plan.pairs + t)], to).start()
        copy(at_ref.at[j], at_ref.at[BC_DEV + j], a_send.at[0], a_recv.at[j], partner).start()

    def send(src, dst, send_sem, recv_sem, i, device):
        for t in range(2):
            copy(src[t].at[i], dst[t], send_sem, recv_sem, device).start()

    def take(recv_sem):
        pltpu.make_async_copy(size_ref.at[0], size_ref.at[0], recv_sem).wait()

    def send_x(i, kind=0):
        send(xs, [r.at[i] for r in xr], x_send.at[kind], x_recv.at[i], i, beside)

    def send_z(u):
        send(zs, [r.at[to_side, u] for r in zr], z_send.at[0], z_recv.at[to_side, u], u, onward)

    def coded_x(i, value):
        encode(value, xs[0].at[i], xs[1].at[i])

    def coded_z(u, value):
        encode(value, zs[0].at[u], zs[1].at[u])

    def from_x(i):
        with jax.named_scope("wait_x"):
            take(x_recv.at[i])
        return decode(xr[0].at[i], xr[1].at[i])

    def from_z(side, u):
        with jax.named_scope("wait_z"):
            take(z_recv.at[side, u])
        return decode(zr[0].at[side, u], zr[1].at[side, u])

    def dot(lhs, b_ref):
        return jnp.dot(lhs, b_ref[...], preferred_element_type=jnp.float32)

    def arrival(ref, n):
        copy(ref, ref, fw_send.at[0], a_recv.at[n], partner).wait_recv()

    def forward(ref, n, size):
        first, second = ref.at[pl.ds(0, size)], ref.at[pl.ds(size, size)]
        with jax.named_scope("wait_a"):
            arrival(first, n)
        copy(first, second, fw_send.at[0], a_recv.at[n + 1], partner).start()

    def forwarded(ref, n, size):
        with jax.named_scope("wait_f"):
            arrival(ref.at[pl.ds(size, size)], n + 1)

    def compute(d):
        @pl.when((d >= BC_DEV) & (d < plan.near))
        def _():
            arrival(at_ref.at[d], d - BC_DEV)

        @pl.when(d >= plan.near)
        def _():
            forwarded(at_ref.at[d], BC_DEV + 2 * (d - plan.near), rows)

        lhs = at_ref[d]
        with jax.named_scope("dot_away"):
            away = dot(lhs, b_away)
            for t in range(2):
                coded_x(2 * d + t, away[t * rows : (t + 1) * rows])
                send_x(2 * d + t)
        with jax.named_scope("dot_own"):
            own = dot(lhs, b_own)
            for t in range(2):
                own_ref[2 * d + t] = own[t * rows : (t + 1) * rows]

    def forward_tail(t):
        forward(tail_ref.at[t], BC_DEV + 2 * (plan.pairs + t), half)

    def compute_tail(t):
        n, i = BC_DEV + 2 * (plan.pairs + t), 2 * plan.slots + t
        forwarded(tail_ref.at[t], n, half)
        lhs = tail_ref[t]
        with jax.named_scope("tail_away"):
            coded_x(i, dot(lhs, b_away))
            send_x(i)
        with jax.named_scope("tail_own"):
            own_ref[i] = dot(lhs, b_own)

        @pl.when(t + 1 < plan.tails)
        def _():
            forward_tail(t + 1)

    def work(s):
        @pl.when((lax.rem(s, 2) == 0) & (s < 2 * plan.slots))
        def _():
            compute(s // 2)

        @pl.when((lax.rem(s, 2) == 1) & (s >= 2 * plan.near - 1) & (s < 2 * plan.slots - 1))
        def _():
            d = (s + 1) // 2
            forward(at_ref.at[d], BC_DEV + 2 * (d - plan.near), rows)

        @pl.when(s == 2 * plan.slots - 1)
        def _():
            forward_tail(0)

        @pl.when((s >= 2 * plan.slots) & (s < plan.units))
        def _():
            compute_tail(s - 2 * plan.slots)

    def fin_send(i):
        def go(src, to_y, to_k, piece, at, size, sem):
            copy(src, land_ref.at[piece, pl.ds(at, size)], f_send.at[0], f_recv.at[sem],
                 (row, col_of(to_y, to_k))).start()

        @pl.when((i >= PIECES) & (i < 2 * PIECES - 1))
        def _():
            go(fin_ref.at[i], y, 1 - k, i - PIECES, 0, rows, i - PIECES)

        @pl.when(i == 2 * PIECES - 1)
        def _():
            for h in range(2):
                go(fin_ref.at[i, pl.ds(h * half, half)], y, 1 - k, PIECES - 1, h * half, half, PIECES - 1 + h)

        @pl.when((i >= 2 * PIECES) & (i < 2 * plan.slots))
        def _():
            q = i // 2 - plan.near
            p, dy = q // plan.others, lax.rem(q, plan.others) + 1
            go(fin_ref.at[i], lax.rem(y + dy, n_y), lax.rem(k + lax.rem(i, 2), PAIR), p, 0, rows, p)

        @pl.when(i >= 2 * plan.slots)
        def _():
            t = i - 2 * plan.slots
            h, dy = t // plan.others, lax.rem(t, plan.others) + 1
            for odd in range(2):
                go(fin_ref.at[i, pl.ds(odd * half, half)], lax.rem(y + dy, n_y), lax.rem(k + odd, PAIR),
                   PIECES - 1, h * half, half, PIECES - 1 + h)

    with jax.named_scope("wait_b"):
        loads[3].wait()
    with jax.named_scope("dot_first"):
        away = dot(at_ref[0], b_away)
        coded_x(0, away[:rows])
        send_x(0)
        away_ref[...] = away[rows:]

        @pl.when(outer)
        def _():
            coded_z(0, away_ref[...])
            send_z(0)

    loads[4].wait()
    with jax.named_scope("dot_first_own"):
        own = dot(at_ref[0], b_own)
        own_ref[0] = own[:rows]
        own_ref[1] = own[rows:]

        @pl.when(outer)
        def _():
            coded_z(1, own_ref[1])
            send_z(1)

    def loop(lag, early, combine):
        def body(s, carry):
            work(s)
            e = s - lag
            if early is not None:
                pl.when(e == 0)(lambda: early(0))
                pl.when(e == 1)(lambda: early(1))

            @pl.when((e >= 2) & (e < plan.hops))
            def _():
                combine(e, jnp.where(e == 2, 0, e - 1))

            return carry

        lax.fori_loop(2, plan.hops + lag, body, 0)

    @pl.when(outer)
    def _():
        def combine(u, i):
            coded_z(u, own_ref[i] + from_x(i))
            send_z(u)

        loop(LAG_OUTER, None, combine)

    @pl.when(inner)
    def _():
        def early(u):
            coded_z(u, (own_ref[1] if u else away_ref[...]) + from_z(from_side, u))
            send_z(u)

        def combine(u, i):
            coded_z(u, own_ref[i] + from_x(i) + from_z(from_side, u))
            send_z(u)

        loop(LAG_INNER, early, combine)

    @pl.when(final)
    def _():
        def early(u):
            total = (own_ref[1] if u else away_ref[...]) + from_z(0, u) + from_z(1, u)
            if u:
                own_ref[1] = total
            else:
                coded_x(1, total)
                send_x(1, 1)

        def combine(u, i):
            total = own_ref[i] + from_x(i) + from_z(0, u) + from_z(1, u)
            fin_ref[i] = total.astype(jnp.bfloat16)
            fin_send(i)

            @pl.when(u == 2 + Z_WAIT)
            def _():
                fin_ref[1] = (own_ref[1] + from_x(1)).astype(jnp.bfloat16)

        loop(LAG_FINAL, early, combine)

    def out(src, p, at, size):
        here = pl.ds(at, size)
        return pltpu.make_async_copy(src.at[p, here], o_ref.at[p, here], out_sem.at[0])

    for p, at, size, sem in [(p, 0, rows, p) for p in range(PIECES - 1)] + [
        (PIECES - 1, h * half, half, PIECES - 1 + h) for h in range(2)
    ]:
        @pl.when(final)
        def _(p=p, at=at, size=size):
            out(fin_ref, p, at, size).start()

        @pl.when(jnp.logical_not(final))
        def _(p=p, at=at, size=size, sem=sem):
            here = land_ref.at[p, pl.ds(at, size)]
            with jax.named_scope("wait_land"):
                copy(here, here, f_send.at[0], f_recv.at[sem], partner).wait_recv()
            out(land_ref, p, at, size).start()

    def drained(ref, sem, t=0):
        pltpu.make_async_copy(ref, ref, sem.at[t]).wait()

    with jax.named_scope("drain"):
        drained(at_ref.at[pl.ds(0, n_y * BC_DEV)], a_send)
        drained(at_ref.at[pl.ds(0, plan.others * BC_DEV)], fw_send)
        drained(size_ref.at[pl.ds(0, plan.units - 1)], x_send)

        @pl.when(jnp.logical_not(final))
        def _():
            drained(size_ref, z_send)

        @pl.when(final)
        def _():
            drained(size_ref.at[0], x_send, 1)
            drained(fin_ref.at[pl.ds(PIECES, plan.units - PIECES)], f_send)

    with jax.named_scope("wait_out"):
        drained(o_ref, out_sem)


def per_device(n_row, n_col, tile_values, tile_counts, tile_cols, panels):
    slots, tile, _ = tile_values.shape
    deep, columns = panels.shape
    wide = columns // PAIR
    plan = Plan(n_col // PAIR)
    rows = BC_DEV * tile // PIECES
    f32, bf16, i16 = jnp.float32, jnp.bfloat16, jnp.int16
    hbm = pl.BlockSpec(memory_space=pl.ANY)
    dma = pltpu.SemaphoreType.DMA

    def coded(*lead):
        return pltpu.VMEM((*lead, rows, wide), i16), pltpu.VMEM((*lead, 1, wide), f32)

    out = pl.pallas_call(
        functools.partial(kernel, n_row, n_col),
        out_shape=pltpu.VMEM((PIECES, rows, wide), bf16),
        in_specs=[hbm] * 4,
        out_specs=pl.BlockSpec(memory_space=pltpu.VMEM),
        scratch_shapes=[
            pltpu.SMEM(tile_counts.shape[::-1], jnp.int32),
            pltpu.SMEM(tile_cols.shape[::-1], jnp.int32),
            pltpu.VMEM((slots, tile, tile), bf16),
            pltpu.VMEM((deep, wide), bf16),
            pltpu.VMEM((deep, wide), bf16),
            pltpu.VMEM((plan.slots, 2 * rows, deep), bf16),
            pltpu.VMEM((plan.tails, rows, deep), bf16),
            pltpu.VMEM((plan.units, rows, wide), f32),
            pltpu.VMEM((rows, wide), f32),
            coded(plan.units),
            coded(plan.units),
            coded(plan.hops),
            coded(2, plan.hops),
            pltpu.VMEM((plan.units, rows, wide), bf16),
            pltpu.VMEM((PIECES, rows, wide), bf16),
            pltpu.VMEM((plan.hops, 1, (rows // 2 + 1) * wide), f32),
            dma((5,)),
            dma((1,)),
            dma((plan.arrivals,)),
            dma((1,)),
            dma((2,)),
            dma((plan.units,)),
            dma((1,)),
            dma((2, plan.hops)),
            dma((1,)),
            dma((PIECES + 1,)),
            dma((1,)),
        ],
        compiler_params=pltpu.CompilerParams(
            collective_id=0, has_side_effects=True, vmem_limit_bytes=56 * 1024 * 1024
        ),
    )(tile_counts.T, tile_cols.T, tile_values, panels)
    return out.reshape(BC_DEV * tile, wide)


def solution(mesh):
    n_row, n_col = mesh.shape["row"], mesh.shape["col"]
    return jax.shard_map(
        functools.partial(per_device, n_row, n_col),
        mesh=mesh,
        in_specs=(P("row", "col", None), P("row", "col"), P("row", "col"), P("row", "col")),
        out_specs=P("col", "row"),
        check_vma=False,
    )
```

time: 44.5 us -> 41.1 us (0.924)
  Pallas kernels: 42.4 us -> 39.6 us
  local copies, waits for them, and re-layouts: 1.67 us -> 0.71 us
    pallas_call x1, Pallas kernels: 42.4 us -> 39.6 us  [per_device(): pl.pallas_call(functools.partial(kernel, n_row, n_col), out_shape=pltpu.V...]
    unnamed x1, local copies, waits for them, and re-layouts: 1.67 us -> 0.71 us
where the time goes in v3:
time: 41.1 us; the launch traced here: 40.4 us
  Pallas kernels  39.6 us (96%)
  local copies, waits for them, and re-layouts  0.71 us (2%)
    pallas_call x1, Pallas kernels, per_device(): pl.pallas_call(functools.partial(kernel, n_row, n_col), out_shape=pltpu.V...  39.6 us

profile of v3, /device:TPU:5, one launch (start us, length us, event | category | flops | bytes accessed | tf_op | source)
XLA Modules:
  0.0 40.4 jit_solution(2416520027577846149)
XLA Ops:
  0.0 39.6 %shard_map.46 = bf16[4,64,512]{2,1,0:T(8,128)(2,1)S(1)} custom-call(s32[1,12]{1,0:T(1,128)} %bitcast.4, s32[1,24]{1,0:T(1,128)} %bitcast.5, bf16[24,128,128]{2,1,0:T(8,128)(2,1)} %tiles_hbm.1, bf16[1536,1024]{1,0:T(8,128)(2,1)} %b_hbm.1), custom_call_target="tpu_custom_call" | custom-call | tf_op jit(solution)/shard_map/pallas_call | solution.py:423
  39.7 0.7 %copy.6 = bf16[256,512]{1,0:T(8,128)(2,1)} copy(bf16[256,512]{1,0:T(8,128)(2,1)S(1)} %bitcast.3) | data formatting | bytes 524288

commit v4 on v3

--- a/solution.py
+++ b/solution.py
@@ -10,7 +10,9 @@
 BC_DEV = 2
 PAIR = 2
 PIECES = 4
+CUTS = 2
 Z_WAIT = 4
+LATE = 2
 LAG_OUTER = 1
 LAG_INNER = 3
 LAG_FINAL = 7
@@ -23,10 +25,11 @@
         self.others = n_y - 1
         self.near = 2 * BC_DEV
         self.pairs = (PIECES - 1) * self.others
-        self.tails = 2 * self.others
+        self.tails = CUTS * self.others
         self.slots = self.near + self.pairs
         self.units = 2 * self.slots + self.tails
         self.hops = self.units + 1
+        self.large = self.hops - self.tails
         self.arrivals = BC_DEV + 2 * (self.pairs + self.tails)
 
 
@@ -57,9 +60,10 @@
 
 def kernel(
     n_row, n_col, counts_hbm, cols_hbm, tiles_hbm, b_hbm, o_ref,
-    counts_ref, cols_ref, tiles_ref, b_away, b_own, at_ref, tail_ref, own_ref, away_ref, xs, xr, zs, zr,
-    fin_ref, land_ref, size_ref, load_sem,
-    a_send, a_recv, fw_send, x_send, x_recv, z_send, z_recv, f_send, f_recv, out_sem,
+    counts_ref, cols_ref, tiles_ref, b_away, b_own, at_ref, tail_ref, own_ref, away_ref, xs, xr, zs, zr, oi,
+    fin_ref, land_ref, size_ref, small_ref, x_size_ref, z_size_ref, large_size_ref,
+    cut_ref, o_size_ref, load_sem,
+    a_send, a_recv, fw_send, x_send, x_recv, z_send, z_recv, o_send, o_recv, f_send, f_recv, out_sem,
 ):
     row, col = lax.axis_index("row"), lax.axis_index("col")
     n_z, n_y = n_row // PAIR, n_col // PAIR
@@ -68,7 +72,8 @@
     y, k = col // PAIR, lax.rem(col, PAIR)
     wide = b_own.shape[1]
     rows = own_ref.shape[1]
-    half = rows // 2
+    cut = rows // CUTS
+    small = 2 * cut
 
     def row_of(z_at, x_at):
         return z_at * PAIR + x_at
@@ -111,6 +116,11 @@
     below = (row_of(jnp.maximum(z - 1, 0), x), col)
     skip_of = (row_of(jnp.where(low_end, 2, n_z - 3), x), col)
 
+    owners = n_z == 4 and n_y == 2
+    owner = owners & (z // 2 != y)
+    owner_row = row_of(jnp.minimum(col, n_z - 1), x)
+    bringer = (row_of(jnp.where(z < 2, 2, 1), x), jnp.minimum(z, n_col - 1))
+
     def flag(b):
         return jnp.where(b, 1, 0).astype(jnp.int32)
 
@@ -126,6 +136,10 @@
     pl.when(z > 0)(lambda: greet(below))
     pl.when(skips)(lambda: greet(onward))
     pl.when(from_skip)(lambda: greet(skip_of))
+    if owners:
+        pl.when(owner)(lambda: greet(bringer))
+        for k_at in range(PAIR):
+            pl.when(inner)(lambda k_at=k_at: greet((owner_row, col_of(1 - y, k_at))))
 
     def copy(src, dst, send, recv, device):
         return pltpu.make_async_remote_copy(
@@ -143,6 +157,7 @@
             with jax.named_scope("wait_barrier"):
                 pl.semaphore_wait(
                     barrier, n_col + flag(z < n_z - 1) + flag(z > 0) + flag(skips) + flag(from_skip)
+                    + (flag(owner) + PAIR * flag(inner) if owners else 0)
                 )
         for p in range(2 * j, 2 * j + 2):
             at = p % 2 * rows
@@ -153,40 +168,56 @@
                     copy(at_ref.at[j, pl.ds(at, rows)], at_ref.at[plan.near + q, pl.ds(0, rows)],
                          a_send.at[0], a_recv.at[BC_DEV + 2 * q], to).start()
                     continue
-                for h in range(2):
+                for h in range(CUTS):
                     t = h * plan.others + dy - 1
-                    copy(at_ref.at[j, pl.ds(at + h * half, half)], tail_ref.at[t, pl.ds(0, half)],
+                    copy(at_ref.at[j, pl.ds(at + h * cut, cut)], tail_ref.at[t, pl.ds(0, cut)],
                          a_send.at[0], a_recv.at[BC_DEV + 2 * (plan.pairs + t)], to).start()
         copy(at_ref.at[j], at_ref.at[BC_DEV + j], a_send.at[0], a_recv.at[j], partner).start()
 
-    def send(src, dst, send_sem, recv_sem, i, device):
-        for t in range(2):
-            copy(src[t].at[i], dst[t], send_sem, recv_sem, device).start()
-
-    def take(recv_sem):
-        pltpu.make_async_copy(size_ref.at[0], size_ref.at[0], recv_sem).wait()
-
-    def send_x(i, kind=0):
-        send(xs, [r.at[i] for r in xr], x_send.at[kind], x_recv.at[i], i, beside)
-
-    def send_z(u):
-        send(zs, [r.at[to_side, u] for r in zr], z_send.at[0], z_recv.at[to_side, u], u, onward)
-
-    def coded_x(i, value):
-        encode(value, xs[0].at[i], xs[1].at[i])
-
-    def coded_z(u, value):
-        encode(value, zs[0].at[u], zs[1].at[u])
-
-    def from_x(i):
+    def first(ref, at, size):
+        return ref.at[at] if size == rows else ref.at[(*at, pl.ds(0, size))]
+
+    def send(src, i, dst, at, size, send_sem, recv_sem, device):
+        copy(first(src[0], (i,), size), first(dst[0], at, size), send_sem, recv_sem, device).start()
+        copy(src[1].at[i], dst[1].at[at], send_sem, recv_sem, device).start()
+
+    def taken(ref, at, size, recv_sem):
+        both = size_ref if size == rows else small_ref
+        pltpu.make_async_copy(both, both, recv_sem).wait()
+        return decode(first(ref[0], at, size), ref[1].at[at])
+
+    def send_x(i, value, kind=0):
+        size = value.shape[0]
+        encode(value, first(xs[0], (i,), size), xs[1].at[i])
+        send(xs, i, xr, (i,), size, x_send.at[kind], x_recv.at[i], beside)
+
+    def code_z(u, value):
+        encode(value, first(zs[0], (u,), value.shape[0]), zs[1].at[u])
+
+    def send_z(u, value):
+        code_z(u, value)
+        send(zs, u, zr, (to_side, u), value.shape[0], z_send.at[0], z_recv.at[to_side, u], onward)
+
+    def send_owners(u, value, which):
+        code_z(u, value)
+        t = u - plan.large
+        for odd in range(PAIR):
+            to = (owner_row, col_of(1 - y, lax.rem(k + odd, PAIR)))
+            for src, dst in ((zs[0].at[u, pl.ds(odd * cut, cut)], oi[0]), (zs[1].at[u], oi[1])):
+                copy(src, dst.at[which, t], o_send.at[0], o_recv.at[which, t], to).start()
+
+    def from_owner(which, t):
+        with jax.named_scope("wait_o"):
+            pltpu.make_async_copy(cut_ref, cut_ref, o_recv.at[which, t]).wait()
+        return decode(oi[0].at[which, t], oi[1].at[which, t])
+
+    def from_x(i, size):
         with jax.named_scope("wait_x"):
-            take(x_recv.at[i])
-        return decode(xr[0].at[i], xr[1].at[i])
-
-    def from_z(side, u):
+            return taken(xr, (i,), size, x_recv.at[i])
+
+    def from_z(side, u, size):
         with jax.named_scope("wait_z"):
-            take(z_recv.at[side, u])
-        return decode(zr[0].at[side, u], zr[1].at[side, u])
+            return taken(zr, (side, u), size, z_recv.at[side, u])
 
     def dot(lhs, b_ref):
         return jnp.dot(lhs, b_ref[...], preferred_element_type=jnp.float32)
@@ -217,29 +248,32 @@
         with jax.named_scope("dot_away"):
             away = dot(lhs, b_away)
             for t in range(2):
-                coded_x(2 * d + t, away[t * rows : (t + 1) * rows])
-                send_x(2 * d + t)
+                send_x(2 * d + t, away[t * rows : (t + 1) * rows])
         with jax.named_scope("dot_own"):
             own = dot(lhs, b_own)
             for t in range(2):
                 own_ref[2 * d + t] = own[t * rows : (t + 1) * rows]
 
     def forward_tail(t):
-        forward(tail_ref.at[t], BC_DEV + 2 * (plan.pairs + t), half)
-
-    def compute_tail(t):
+        forward(tail_ref.at[t], BC_DEV + 2 * (plan.pairs + t), cut)
+
+    def tail_away(t):
         n, i = BC_DEV + 2 * (plan.pairs + t), 2 * plan.slots + t
-        forwarded(tail_ref.at[t], n, half)
-        lhs = tail_ref[t]
+
+        @pl.when(t + 1 < plan.tails)
+        def _():
+            forward_tail(t + 1)
+
+        forwarded(tail_ref.at[t], n, cut)
         with jax.named_scope("tail_away"):
-            coded_x(i, dot(lhs, b_away))
-            send_x(i)
+            send_x(i, dot(tail_ref[t], b_away))
+
+    def tail_own(g):
+        both = tail_ref[pl.ds(2 * g, 2)].reshape(2 * small, tail_ref.shape[2])
         with jax.named_scope("tail_own"):
-            own_ref[i] = dot(lhs, b_own)
-
-        @pl.when(t + 1 < plan.tails)
-        def _():
-            forward_tail(t + 1)
+            own = dot(both, b_own)
+            for t in range(2):
+                own_ref[2 * plan.slots + 2 * g + t, pl.ds(0, small)] = own[t * small : (t + 1) * small]
 
     def work(s):
         @pl.when((lax.rem(s, 2) == 0) & (s < 2 * plan.slots))
@@ -251,54 +285,62 @@
             d = (s + 1) // 2
             forward(at_ref.at[d], BC_DEV + 2 * (d - plan.near), rows)
 
-        @pl.when(s == 2 * plan.slots - 1)
+        m = s - (2 * plan.slots - 1)
+
+        @pl.when(m == 0)
         def _():
             forward_tail(0)
-
-        @pl.when((s >= 2 * plan.slots) & (s < plan.units))
-        def _():
-            compute_tail(s - 2 * plan.slots)
-
-    def fin_send(i):
+            tail_away(0)
+
+        @pl.when((m >= 1) & (2 * m <= plan.tails))
+        def _():
+            tail_away(2 * m - 1)
+            tail_own(m - 1)
+
+        @pl.when((m >= 1) & (2 * m < plan.tails))
+        def _():
+            tail_away(2 * m)
+
+    def fin_send(i, tail):
         def go(src, to_y, to_k, piece, at, size, sem):
             copy(src, land_ref.at[piece, pl.ds(at, size)], f_send.at[0], f_recv.at[sem],
                  (row, col_of(to_y, to_k))).start()
 
+        def cuts(h, src, at, to_y, to_k):
+            go(src.at[i, pl.ds(at, cut)], to_y, to_k, PIECES - 1, h * cut, cut, PIECES - 1 + h)
+
+        if tail:
+            t = i - 2 * plan.slots
+            h, dy = t // plan.others, lax.rem(t, plan.others) + 1
+            for odd in range(2):
+                cuts(h, fin_ref, odd * cut, lax.rem(y + dy, n_y), lax.rem(k + odd, PAIR))
+            return
+
         @pl.when((i >= PIECES) & (i < 2 * PIECES - 1))
         def _():
             go(fin_ref.at[i], y, 1 - k, i - PIECES, 0, rows, i - PIECES)
 
         @pl.when(i == 2 * PIECES - 1)
         def _():
-            for h in range(2):
-                go(fin_ref.at[i, pl.ds(h * half, half)], y, 1 - k, PIECES - 1, h * half, half, PIECES - 1 + h)
-
-        @pl.when((i >= 2 * PIECES) & (i < 2 * plan.slots))
+            for h in range(CUTS):
+                cuts(h, fin_ref, h * cut, y, 1 - k)
+
+        @pl.when(i >= 2 * PIECES)
         def _():
             q = i // 2 - plan.near
             p, dy = q // plan.others, lax.rem(q, plan.others) + 1
             go(fin_ref.at[i], lax.rem(y + dy, n_y), lax.rem(k + lax.rem(i, 2), PAIR), p, 0, rows, p)
-
-        @pl.when(i >= 2 * plan.slots)
-        def _():
-            t = i - 2 * plan.slots
-            h, dy = t // plan.others, lax.rem(t, plan.others) + 1
-            for odd in range(2):
-                go(fin_ref.at[i, pl.ds(odd * half, half)], lax.rem(y + dy, n_y), lax.rem(k + odd, PAIR),
-                   PIECES - 1, h * half, half, PIECES - 1 + h)
 
     with jax.named_scope("wait_b"):
         loads[3].wait()
     with jax.named_scope("dot_first"):
         away = dot(at_ref[0], b_away)
-        coded_x(0, away[:rows])
-        send_x(0)
+        send_x(0, away[:rows])
         away_ref[...] = away[rows:]
 
         @pl.when(outer)
         def _():
-            coded_z(0, away_ref[...])
-            send_z(0)
+            send_z(0, away_ref[...])
 
     loads[4].wait()
     with jax.named_scope("dot_first_own"):
@@ -308,10 +350,9 @@
 
         @pl.when(outer)
         def _():
-            coded_z(1, own_ref[1])
-            send_z(1)
-
-    def loop(lag, early, combine):
+            send_z(1, own_ref[1])
+
+    def loop(lag, early, combine, late=0):
         def body(s, carry):
             work(s)
             e = s - lag
@@ -319,92 +360,130 @@
                 pl.when(e == 0)(lambda: early(0))
                 pl.when(e == 1)(lambda: early(1))
 
-            @pl.when((e >= 2) & (e < plan.hops))
+            tails_at = plan.large - late
+            tail = (e >= tails_at) & (e < tails_at + plan.tails)
+
+            @pl.when((e >= 2) & (e < plan.hops) & jnp.logical_not(tail))
             def _():
-                combine(e, jnp.where(e == 2, 0, e - 1))
+                u = jnp.where(e < tails_at, e, e - plan.tails)
+                combine(u, jnp.where(u == 2, 0, u - 1), rows, False)
+
+            @pl.when(tail)
+            def _():
+                combine(e + late, e + late - 1, small, True)
 
             return carry
 
         lax.fori_loop(2, plan.hops + lag, body, 0)
+
+    def own(i, size):
+        return first(own_ref, (i,), size)[...]
 
     @pl.when(outer)
     def _():
-        def combine(u, i):
-            coded_z(u, own_ref[i] + from_x(i))
-            send_z(u)
+        def combine(u, i, size, tail):
+            send_z(u, own(i, size) + from_x(i, size))
 
         loop(LAG_OUTER, None, combine)
 
     @pl.when(inner)
     def _():
         def early(u):
-            coded_z(u, (own_ref[1] if u else away_ref[...]) + from_z(from_side, u))
-            send_z(u)
-
-        def combine(u, i):
-            coded_z(u, own_ref[i] + from_x(i) + from_z(from_side, u))
-            send_z(u)
+            send_z(u, (own_ref[1] if u else away_ref[...]) + from_z(from_side, u, rows))
+
+        def combine(u, i, size, tail):
+            total = own(i, size) + from_x(i, size) + from_z(from_side, u, size)
+            if tail and owners:
+                send_owners(u, total, 0)
+            else:
+                send_z(u, total)
 
         loop(LAG_INNER, early, combine)
 
     @pl.when(final)
     def _():
         def early(u):
-            total = (own_ref[1] if u else away_ref[...]) + from_z(0, u) + from_z(1, u)
+            total = (own_ref[1] if u else away_ref[...]) + from_z(0, u, rows) + from_z(1, u, rows)
             if u:
                 own_ref[1] = total
             else:
-                coded_x(1, total)
-                send_x(1, 1)
-
-        def combine(u, i):
-            total = own_ref[i] + from_x(i) + from_z(0, u) + from_z(1, u)
-            fin_ref[i] = total.astype(jnp.bfloat16)
-            fin_send(i)
-
-            @pl.when(u == 2 + Z_WAIT)
-            def _():
-                fin_ref[1] = (own_ref[1] + from_x(1)).astype(jnp.bfloat16)
-
-        loop(LAG_FINAL, early, combine)
+                send_x(1, total, 1)
+
+        def combine(u, i, size, tail):
+            total = own(i, size) + from_x(i, size)
+            if tail and owners:
+                send_owners(u, total + from_z(k, u, size), 1)
+                return
+            total += from_z(0, u, size) + from_z(1, u, size)
+            first(fin_ref, (i,), size)[...] = total.astype(jnp.bfloat16)
+            fin_send(i, tail)
+
+            if not tail:
+                @pl.when(u == 2 + Z_WAIT)
+                def _():
+                    fin_ref[1] = (own_ref[1] + from_x(1, rows)).astype(jnp.bfloat16)
+
+        loop(LAG_FINAL, early, combine, LATE if owners else 0)
 
     def out(src, p, at, size):
         here = pl.ds(at, size)
         return pltpu.make_async_copy(src.at[p, here], o_ref.at[p, here], out_sem.at[0])
 
-    for p, at, size, sem in [(p, 0, rows, p) for p in range(PIECES - 1)] + [
-        (PIECES - 1, h * half, half, PIECES - 1 + h) for h in range(2)
-    ]:
+    def hand_over(p, at, size, sem):
         @pl.when(final)
-        def _(p=p, at=at, size=size):
+        def _():
             out(fin_ref, p, at, size).start()
 
         @pl.when(jnp.logical_not(final))
-        def _(p=p, at=at, size=size, sem=sem):
+        def _():
             here = land_ref.at[p, pl.ds(at, size)]
             with jax.named_scope("wait_land"):
                 copy(here, here, f_send.at[0], f_recv.at[sem], partner).wait_recv()
             out(land_ref, p, at, size).start()
 
+    def hand_over_cuts():
+        for h in range(CUTS):
+            hand_over(PIECES - 1, h * cut, cut, PIECES - 1 + h)
+
+    for p in range(PIECES - 1):
+        hand_over(p, 0, rows, p)
+    if owners:
+        pl.when(jnp.logical_not(owner))(hand_over_cuts)
+
+        @pl.when(owner)
+        def _():
+            for t in range(CUTS):
+                o_ref[PIECES - 1, pl.ds(t * cut, cut)] = (from_owner(1, t) + from_owner(0, t)).astype(jnp.bfloat16)
+    else:
+        hand_over_cuts()
+
     def drained(ref, sem, t=0):
         pltpu.make_async_copy(ref, ref, sem.at[t]).wait()
 
     with jax.named_scope("drain"):
         drained(at_ref.at[pl.ds(0, n_y * BC_DEV)], a_send)
         drained(at_ref.at[pl.ds(0, plan.others * BC_DEV)], fw_send)
-        drained(size_ref.at[pl.ds(0, plan.units - 1)], x_send)
-
-        @pl.when(jnp.logical_not(final))
-        def _():
-            drained(size_ref, z_send)
+        drained(x_size_ref, x_send)
+
+        if owners:
+            pl.when(outer)(lambda: drained(z_size_ref, z_send))
+            pl.when(inner)(lambda: drained(large_size_ref, z_send))
+            pl.when(jnp.logical_not(outer))(lambda: drained(o_size_ref, o_send))
+        else:
+            pl.when(jnp.logical_not(final))(lambda: drained(z_size_ref, z_send))
 
         @pl.when(final)
         def _():
-            drained(size_ref.at[0], x_send, 1)
-            drained(fin_ref.at[pl.ds(PIECES, plan.units - PIECES)], f_send)
+            drained(size_ref, x_send, 1)
+            sent = 2 * plan.slots if owners else PIECES * n_col
+            drained(fin_ref.at[pl.ds(PIECES, sent - PIECES)], f_send)
 
     with jax.named_scope("wait_out"):
-        drained(o_ref, out_sem)
+        if owners:
+            pl.when(owner)(lambda: drained(o_ref.at[pl.ds(0, PIECES - 1)], out_sem))
+            pl.when(jnp.logical_not(owner))(lambda: drained(o_ref, out_sem))
+        else:
+            drained(o_ref, out_sem)
 
 
 def per_device(n_row, n_col, tile_values, tile_counts, tile_cols, panels):
@@ -413,12 +492,16 @@
     wide = columns // PAIR
     plan = Plan(n_col // PAIR)
     rows = BC_DEV * tile // PIECES
+    cut = rows // CUTS
     f32, bf16, i16 = jnp.float32, jnp.bfloat16, jnp.int16
     hbm = pl.BlockSpec(memory_space=pl.ANY)
     dma = pltpu.SemaphoreType.DMA
 
     def coded(*lead):
         return pltpu.VMEM((*lead, rows, wide), i16), pltpu.VMEM((*lead, 1, wide), f32)
+
+    def words(large, small):
+        return pltpu.VMEM((1, (large * (rows // 2 + 1) + small * (rows // CUTS + 1)) * wide), f32)
 
     out = pl.pallas_call(
         functools.partial(kernel, n_row, n_col),
@@ -432,16 +515,23 @@
             pltpu.VMEM((deep, wide), bf16),
             pltpu.VMEM((deep, wide), bf16),
             pltpu.VMEM((plan.slots, 2 * rows, deep), bf16),
-            pltpu.VMEM((plan.tails, rows, deep), bf16),
+            pltpu.VMEM((plan.tails, 2 * rows // CUTS, deep), bf16),
             pltpu.VMEM((plan.units, rows, wide), f32),
             pltpu.VMEM((rows, wide), f32),
             coded(plan.units),
             coded(plan.units),
             coded(plan.hops),
             coded(2, plan.hops),
+            (pltpu.VMEM((2, CUTS, cut, wide), i16), pltpu.VMEM((2, CUTS, 1, wide), f32)),
             pltpu.VMEM((plan.units, rows, wide), bf16),
             pltpu.VMEM((PIECES, rows, wide), bf16),
-            pltpu.VMEM((plan.hops, 1, (rows // 2 + 1) * wide), f32),
+            words(1, 0),
+            words(0, 1),
+            words(plan.large - 2, plan.tails),
+            words(plan.large, plan.tails),
+            words(plan.large, 0),
+            pltpu.VMEM((1, (cut // 2 + 1) * wide), f32),
+            pltpu.VMEM((1, PAIR * CUTS * (cut // 2 + 1) * wide), f32),
             dma((5,)),
             dma((1,)),
             dma((plan.arrivals,)),
@@ -451,7 +541,9 @@
             dma((1,)),
             dma((2, plan.hops)),
             dma((1,)),
-            dma((PIECES + 1,)),
+            dma((2, CUTS)),
+            dma((1,)),
+            dma((PIECES - 1 + CUTS,)),
             dma((1,)),
         ],
         compiler_params=pltpu.CompilerParams(

time: 41.1 us -> 40 us (0.973)
  Pallas kernels: 39.6 us -> 38.8 us
    pallas_call x1, Pallas kernels: 39.6 us -> 38.8 us  [per_device(): pl.pallas_call(functools.partial(kernel, n_row, n_col), out_shape=pltpu.V...]
where the time goes in v4:
time: 40 us; the launch traced here: 39.5 us
  Pallas kernels  38.8 us (97%)
  local copies, waits for them, and re-layouts  0.71 us (2%)
    pallas_call x1, Pallas kernels, per_device(): pl.pallas_call(functools.partial(kernel, n_row, n_col), out_shape=pltpu.V...  38.8 us

profile of v4, /device:TPU:5, one launch (start us, length us, event | category | flops | bytes accessed | tf_op | source)
XLA Modules:
  0.0 39.5 jit_solution(6567745868473496296)
XLA Ops:
  0.0 38.8 %shard_map.46 = bf16[4,64,512]{2,1,0:T(8,128)(2,1)S(1)} custom-call(s32[1,12]{1,0:T(1,128)} %bitcast.4, s32[1,24]{1,0:T(1,128)} %bitcast.5, bf16[24,128,128]{2,1,0:T(8,128)(2,1)} %tiles_hbm.1, bf16[1536,1024]{1,0:T(8,128)(2,1)} %b_hbm.1), custom_call_target="tpu_custom_call" | custom-call | tf_op jit(solution)/shard_map/pallas_call | solution.py:506
  38.8 0.7 %copy.6 = bf16[256,512]{1,0:T(8,128)(2,1)} copy(bf16[256,512]{1,0:T(8,128)(2,1)S(1)} %bitcast.3) | data formatting | bytes 524288

commit v5 on v4

--- a/solution.py
+++ b/solution.py
@@ -12,7 +12,7 @@
 PIECES = 4
 CUTS = 2
 Z_WAIT = 4
-LATE = 2
+LATE = 5
 LAG_OUTER = 1
 LAG_INNER = 3
 LAG_FINAL = 7
@@ -60,10 +60,10 @@
 
 def kernel(
     n_row, n_col, counts_hbm, cols_hbm, tiles_hbm, b_hbm, o_ref,
-    counts_ref, cols_ref, tiles_ref, b_away, b_own, at_ref, tail_ref, own_ref, away_ref, xs, xr, zs, zr, oi,
+    counts_ref, cols_ref, tiles_ref, b_away, b_own, at_ref, tail_ref, own_ref, away_ref, xs, xr, zs, zr, part,
     fin_ref, land_ref, size_ref, small_ref, x_size_ref, z_size_ref, large_size_ref,
-    cut_ref, o_size_ref, load_sem,
-    a_send, a_recv, fw_send, x_send, x_recv, z_send, z_recv, o_send, o_recv, f_send, f_recv, out_sem,
+    parts_size_ref, load_sem,
+    a_send, a_recv, fw_send, x_send, x_recv, z_send, z_recv, p_recv, f_send, f_recv, out_sem,
 ):
     row, col = lax.axis_index("row"), lax.axis_index("col")
     n_z, n_y = n_row // PAIR, n_col // PAIR
@@ -118,8 +118,12 @@
 
     owners = n_z == 4 and n_y == 2
     owner = owners & (z // 2 != y)
+    near = outer & (z // 2 == y)
     owner_row = row_of(jnp.minimum(col, n_z - 1), x)
     bringer = (row_of(jnp.where(z < 2, 2, 1), x), jnp.minimum(z, n_col - 1))
+    inner_of = (row_of(jnp.where(y == 0, 2, 1), x), col)
+    apart = (col == 1) & ((z == 0) | (z == 2)) | (col == 2) & ((z == 3) | (z == 1))
+    apart_from = (row_of(jnp.clip(2 * col - z, 0, n_z - 1), x), col)
 
     def flag(b):
         return jnp.where(b, 1, 0).astype(jnp.int32)
@@ -138,6 +142,7 @@
     pl.when(from_skip)(lambda: greet(skip_of))
     if owners:
         pl.when(owner)(lambda: greet(bringer))
+        pl.when(apart)(lambda: greet(apart_from))
         for k_at in range(PAIR):
             pl.when(inner)(lambda k_at=k_at: greet((owner_row, col_of(1 - y, k_at))))
 
@@ -150,14 +155,14 @@
     with jax.named_scope("wait_tiles"):
         for c in loads[:3]:
             c.wait()
-    for j in range(BC_DEV):
+    def prepare(j):
         with jax.named_scope("build"):
             build_dense(j, counts_ref, cols_ref, tiles_ref, at_ref)
         if j == 0:
             with jax.named_scope("wait_barrier"):
                 pl.semaphore_wait(
                     barrier, n_col + flag(z < n_z - 1) + flag(z > 0) + flag(skips) + flag(from_skip)
-                    + (flag(owner) + PAIR * flag(inner) if owners else 0)
+                    + (flag(owner) + flag(apart) + PAIR * flag(inner) if owners else 0)
                 )
         for p in range(2 * j, 2 * j + 2):
             at = p % 2 * rows
@@ -174,6 +179,8 @@
                          a_send.at[0], a_recv.at[BC_DEV + 2 * (plan.pairs + t)], to).start()
         copy(at_ref.at[j], at_ref.at[BC_DEV + j], a_send.at[0], a_recv.at[j], partner).start()
 
+    prepare(0)
+
     def first(ref, at, size):
         return ref.at[at] if size == rows else ref.at[(*at, pl.ds(0, size))]
 
@@ -198,18 +205,13 @@
         code_z(u, value)
         send(zs, u, zr, (to_side, u), value.shape[0], z_send.at[0], z_recv.at[to_side, u], onward)
 
-    def send_owners(u, value, which):
+    def send_part(u, value, which):
         code_z(u, value)
-        t = u - plan.large
-        for odd in range(PAIR):
-            to = (owner_row, col_of(1 - y, lax.rem(k + odd, PAIR)))
-            for src, dst in ((zs[0].at[u, pl.ds(odd * cut, cut)], oi[0]), (zs[1].at[u], oi[1])):
-                copy(src, dst.at[which, t], o_send.at[0], o_recv.at[which, t], to).start()
-
-    def from_owner(which, t):
-        with jax.named_scope("wait_o"):
-            pltpu.make_async_copy(cut_ref, cut_ref, o_recv.at[which, t]).wait()
-        return decode(oi[0].at[which, t], oi[1].at[which, t])
+        send(zs, u, part, (which, u - plan.large), small, z_send.at[0], p_recv.at[which, u - plan.large], inner_of)
+
+    def from_part(which, u):
+        with jax.named_scope("wait_p"):
+            return taken(part, (which, u - plan.large), small, p_recv.at[which, u - plan.large])
 
     def from_x(i, size):
         with jax.named_scope("wait_x"):
@@ -304,7 +306,7 @@
     def fin_send(i, tail):
         def go(src, to_y, to_k, piece, at, size, sem):
             copy(src, land_ref.at[piece, pl.ds(at, size)], f_send.at[0], f_recv.at[sem],
-                 (row, col_of(to_y, to_k))).start()
+                 (owner_row if tail and owners else row, col_of(to_y, to_k))).start()
 
         def cuts(h, src, at, to_y, to_k):
             go(src.at[i, pl.ds(at, cut)], to_y, to_k, PIECES - 1, h * cut, cut, PIECES - 1 + h)
@@ -335,13 +337,11 @@
         loads[3].wait()
     with jax.named_scope("dot_first"):
         away = dot(at_ref[0], b_away)
+        away_ref[...] = away[rows:]
+        pl.when(outer)(lambda: send_z(0, away_ref[...]))
         send_x(0, away[:rows])
-        away_ref[...] = away[rows:]
-
-        @pl.when(outer)
-        def _():
-            send_z(0, away_ref[...])
-
+
+    prepare(1)
     loads[4].wait()
     with jax.named_scope("dot_first_own"):
         own = dot(at_ref[0], b_own)
@@ -382,7 +382,12 @@
     @pl.when(outer)
     def _():
         def combine(u, i, size, tail):
-            send_z(u, own(i, size) + from_x(i, size))
+            total = own(i, size) + from_x(i, size)
+            if not (tail and owners):
+                send_z(u, total)
+                return
+            pl.when(near)(lambda: send_part(u, total, 0))
+            pl.when(jnp.logical_not(near))(lambda: send_z(u, total))
 
         loop(LAG_OUTER, None, combine)
 
@@ -393,10 +398,12 @@
 
         def combine(u, i, size, tail):
             total = own(i, size) + from_x(i, size) + from_z(from_side, u, size)
-            if tail and owners:
-                send_owners(u, total, 0)
-            else:
+            if not (tail and owners):
                 send_z(u, total)
+                return
+            total += from_part(0, u) + from_part(1, u)
+            first(fin_ref, (i,), size)[...] = total.astype(jnp.bfloat16)
+            fin_send(i, tail)
 
         loop(LAG_INNER, early, combine)
 
@@ -412,7 +419,7 @@
         def combine(u, i, size, tail):
             total = own(i, size) + from_x(i, size)
             if tail and owners:
-                send_owners(u, total + from_z(k, u, size), 1)
+                send_part(u, total, 1)
                 return
             total += from_z(0, u, size) + from_z(1, u, size)
             first(fin_ref, (i,), size)[...] = total.astype(jnp.bfloat16)
@@ -447,15 +454,7 @@
 
     for p in range(PIECES - 1):
         hand_over(p, 0, rows, p)
-    if owners:
-        pl.when(jnp.logical_not(owner))(hand_over_cuts)
-
-        @pl.when(owner)
-        def _():
-            for t in range(CUTS):
-                o_ref[PIECES - 1, pl.ds(t * cut, cut)] = (from_owner(1, t) + from_owner(0, t)).astype(jnp.bfloat16)
-    else:
-        hand_over_cuts()
+    hand_over_cuts()
 
     def drained(ref, sem, t=0):
         pltpu.make_async_copy(ref, ref, sem.at[t]).wait()
@@ -467,8 +466,12 @@
 
         if owners:
             pl.when(outer)(lambda: drained(z_size_ref, z_send))
-            pl.when(inner)(lambda: drained(large_size_ref, z_send))
-            pl.when(jnp.logical_not(outer))(lambda: drained(o_size_ref, o_send))
+            pl.when(final)(lambda: drained(parts_size_ref, z_send))
+
+            @pl.when(inner)
+            def _():
+                drained(large_size_ref, z_send)
+                drained(fin_ref.at[pl.ds(0, plan.tails * small // rows)], f_send)
         else:
             pl.when(jnp.logical_not(final))(lambda: drained(z_size_ref, z_send))
 
@@ -479,11 +482,7 @@
             drained(fin_ref.at[pl.ds(PIECES, sent - PIECES)], f_send)
 
     with jax.named_scope("wait_out"):
-        if owners:
-            pl.when(owner)(lambda: drained(o_ref.at[pl.ds(0, PIECES - 1)], out_sem))
-            pl.when(jnp.logical_not(owner))(lambda: drained(o_ref, out_sem))
-        else:
-            drained(o_ref, out_sem)
+        drained(o_ref, out_sem)
 
 
 def per_device(n_row, n_col, tile_values, tile_counts, tile_cols, panels):
@@ -492,7 +491,6 @@
     wide = columns // PAIR
     plan = Plan(n_col // PAIR)
     rows = BC_DEV * tile // PIECES
-    cut = rows // CUTS
     f32, bf16, i16 = jnp.float32, jnp.bfloat16, jnp.int16
     hbm = pl.BlockSpec(memory_space=pl.ANY)
     dma = pltpu.SemaphoreType.DMA
@@ -522,7 +520,7 @@
             coded(plan.units),
             coded(plan.hops),
             coded(2, plan.hops),
-            (pltpu.VMEM((2, CUTS, cut, wide), i16), pltpu.VMEM((2, CUTS, 1, wide), f32)),
+            coded(2, plan.tails),
             pltpu.VMEM((plan.units, rows, wide), bf16),
             pltpu.VMEM((PIECES, rows, wide), bf16),
             words(1, 0),
@@ -530,8 +528,7 @@
             words(plan.large - 2, plan.tails),
             words(plan.large, plan.tails),
             words(plan.large, 0),
-            pltpu.VMEM((1, (cut // 2 + 1) * wide), f32),
-            pltpu.VMEM((1, PAIR * CUTS * (cut // 2 + 1) * wide), f32),
+            words(0, plan.tails),
             dma((5,)),
             dma((1,)),
             dma((plan.arrivals,)),
@@ -540,8 +537,7 @@
             dma((plan.units,)),
             dma((1,)),
             dma((2, plan.hops)),
-            dma((1,)),
-            dma((2, CUTS)),
+            dma((2, plan.tails)),
             dma((1,)),
             dma((PIECES - 1 + CUTS,)),
             dma((1,)),

time: 40 us -> 39.5 us (0.988)
  no operation moved by 1% of the time
where the time goes in v5:
time: 39.5 us; the launch traced here: 39.4 us
  Pallas kernels  38.6 us (98%)
  local copies, waits for them, and re-layouts  0.71 us (2%)
    pallas_call x1, Pallas kernels, per_device(): pl.pallas_call(functools.partial(kernel, n_row, n_col), out_shape=pltpu.V...  38.6 us

profile of v5, /device:TPU:5, one launch (start us, length us, event | category | flops | bytes accessed | tf_op | source)
XLA Modules:
  0.0 39.4 jit_solution(14510461106256159282)
XLA Ops:
  0.0 38.6 %shard_map.46 = bf16[4,64,512]{2,1,0:T(8,128)(2,1)S(1)} custom-call(s32[1,12]{1,0:T(1,128)} %bitcast.4, s32[1,24]{1,0:T(1,128)} %bitcast.5, bf16[24,128,128]{2,1,0:T(8,128)(2,1)} %tiles_hbm.1, bf16[1536,1024]{1,0:T(8,128)(2,1)} %b_hbm.1), custom_call_target="tpu_custom_call" | custom-call | tf_op jit(solution)/shard_map/pallas_call | solution.py:504
  38.7 0.7 %copy.6 = bf16[256,512]{1,0:T(8,128)(2,1)} copy(bf16[256,512]{1,0:T(8,128)(2,1)S(1)} %bitcast.3) | data formatting | bytes 524288

commit v6 on v5

--- a/solution.py
+++ b/solution.py
@@ -10,9 +10,9 @@
 BC_DEV = 2
 PAIR = 2
 PIECES = 4
-CUTS = 2
+CUTS = 4
 Z_WAIT = 4
-LATE = 5
+LATE = 4
 LAG_OUTER = 1
 LAG_INNER = 3
 LAG_FINAL = 7

time: 39.5 us -> 39.5 us (level)
  no operation moved by 1% of the time
where the time goes in v6:
time: 39.5 us; the launch traced here: 39.3 us
  Pallas kernels  38.6 us (98%)
  local copies, waits for them, and re-layouts  0.71 us (2%)
    pallas_call x1, Pallas kernels, per_device(): pl.pallas_call(functools.partial(kernel, n_row, n_col), out_shape=pltpu.V...  38.6 us

profile of v6, /device:TPU:5, one launch (start us, length us, event | category | flops | bytes accessed | tf_op | source)
XLA Modules:
  0.0 39.3 jit_solution(16785008058597005731)
XLA Ops:
  0.0 38.6 %shard_map.46 = bf16[4,64,512]{2,1,0:T(8,128)(2,1)S(1)} custom-call(s32[1,12]{1,0:T(1,128)} %bitcast.4, s32[1,24]{1,0:T(1,128)} %bitcast.5, bf16[24,128,128]{2,1,0:T(8,128)(2,1)} %tiles_hbm.1, bf16[1536,1024]{1,0:T(8,128)(2,1)} %b_hbm.1), custom_call_target="tpu_custom_call" | custom-call | tf_op jit(solution)/shard_map/pallas_call | solution.py:504
  38.6 0.7 %copy.6 = bf16[256,512]{1,0:T(8,128)(2,1)} copy(bf16[256,512]{1,0:T(8,128)(2,1)S(1)} %bitcast.3) | data formatting | bytes 524288
